TPU v7x, 32 devices: a whole 2x2x4 slice. The times are simulated.
32 devices in a mesh: dap: 8 (over z, x), cplx: 4 (over y, core).
Axes of the slice: x: 2, y: 2, z: 4, core: 2. Of those that a mesh axis runs over, the one named last changes fastest.
Arguments:
- pair: bfloat16 [96, 384, 128], P('dap', 'cplx'), parts along dimension 1, may hold values from -6 to 6
- cotangent: bfloat16 [96, 384, 128], P('dap', 'cplx'), parts along dimension 1, may hold values from -6 to 6
- residue_mask: int32 [384], P('cplx'), parts along dimension 0, may hold values 0 or 1
- chain_ids: int32 [384], P('cplx'), parts along dimension 0, may hold values from 0 to 2, never falling along the last dimension, each value on 1 to 48 neighbouring positions
- chain_embed: float32 [2, 128], replicated, may hold values from -4 to 4
- out_norm_gain: float32 [128], replicated, may hold values from 0.25 to 1.75
- out_proj: bfloat16 [128, 512], replicated, may hold values from -0.5 to 0.5
- out_gate: bfloat16 [128, 128], replicated, may hold values from -0.5 to 0.5
- out_mid_gain: float32 [128], replicated, may hold values from 0.25 to 1.75
- out_final: bfloat16 [128, 128], replicated, may hold values from -0.5 to 0.5
- in_norm_gain: float32 [128], replicated, may hold values from 0.25 to 1.75
- in_proj: bfloat16 [128, 512], replicated, may hold values from -0.5 to 0.5
- in_gate: bfloat16 [128, 128], replicated, may hold values from -0.5 to 0.5
- in_mid_gain: float32 [128], replicated, may hold values from 0.25 to 1.75
- in_final: bfloat16 [128, 128], replicated, may hold values from -0.5 to 0.5
Outputs:
- pair_grad: bfloat16 [96, 384, 128], P('dap', 'cplx'), parts along dimension 1
- grad_proj: float32 [512, 512], P('cplx'), parts along dimension 0
- grad_gate: float32 [512, 128], P('cplx'), parts along dimension 0
- grad_final: float32 [512, 128], P('cplx'), parts along dimension 0
- grad_norm_gain: float32 [512], P('cplx'), parts along dimension 0
- grad_mid_gain: float32 [512], P('cplx'), parts along dimension 0
There are 4 independent parts, one for each index of `cplx`. A program takes and returns all parts, laid end to end along the dimension named above; an argument that names none is the same for every part. Nothing has to cross between parts.
Inputs may be any that keep to these rules, and one draw needn't show every extreme that they name: `chain_ids`: chain numbers never fall along the residues; each chain has at most 48 residues.
All inputs are finite; a program needn't handle non-finite values.
Results may differ from a plain program's by a relative error of at most 0.019.
Values may be sent and summed in bfloat16 or wider, within the bound.
A program may use at most 128 MiB of HBM per device.

v0:
```python
import functools

import jax
import jax.numpy as jnp
from jax import lax
from jax.experimental import pallas as pl
from jax.experimental.pallas import tpu as pltpu
from jax.sharding import PartitionSpec as P

F32 = jnp.float32
BF16 = jnp.bfloat16
LANES = 128
A_OUT, B_OUT, X_OUT, A_IN, B_IN, X_IN, G_X, G_A, G_B, P_SUM, P_ALL, H_SUM, H_ALL, GAINS = range(14)


def tn(w, x):
    return lax.dot_general(w, x, (((0,), (0,)), ((), ())), preferred_element_type=F32)


def nn(w, x):
    return jnp.dot(w, x, preferred_element_type=F32)


def nt(w, x):
    return lax.dot_general(w, x, (((1,), (1,)), ((), ())), preferred_element_type=F32)


def sigmoid(v):
    return 1.0 / (1.0 + jnp.exp(-v))


def norm_stats(v):
    centred = v - jnp.mean(v, axis=0, keepdims=True)
    inv = lax.rsqrt(jnp.mean(centred * centred, axis=0, keepdims=True) + 1e-05)
    return centred * inv, inv


def norm_back(grad, hat, inv, gain):
    scaled = grad * gain
    m1 = jnp.mean(scaled, axis=0, keepdims=True)
    m2 = jnp.mean(scaled * hat, axis=0, keepdims=True)
    return inv * (scaled - m1 - hat * m2)


def lane_sum(v):
    return jnp.sum(v, axis=1, keepdims=True)


def kernel(
    n, rows, res, lc,
    pair, cot, residues, chains, embed, gain_on, gain_om, gain_in, gain_im, out_proj, out_gate, out_final, in_proj, in_gate, in_final,
    grad_out, gp_out, gg_out, gf_out, gn_out, gm_out,
    cols, masks, in_q, start, normed, gate, in_p, cot_t, mid, logit_s, gv, gy, gl,
    a_s, b_s, x_s, a_r, b_r, x_r,
    a2_s, b2_s, x2_s, a2_r, b2_r, x2_r,
    gx_s, gx_r, ga_s, gb_s, ga_r, gb_r,
    slab_a, slab_b, slab_o, slab_p, mat_a, mat_b, mat_x,
    acc_p, acc_g, acc_f, acc_n, acc_m, g_s, g_r, t_s, t_r, h_s, h_r, u_s, u_r, w_s, w_r,
    send_sem, recv_sem,
):
    me = lax.axis_index("dap")
    c = start.shape[0]
    per = c // n
    total = rows * res
    chunks = total // lc
    crows = lc // res
    tiles = -(-res // LANES)
    inv_count = 1.0 / res

    barrier = pltpu.get_barrier_semaphore()
    for p in range(1, n):
        pl.semaphore_signal(
            barrier, inc=1, device_id={"dap": lax.rem(me + p, n)},
            device_id_type=pl.DeviceIdType.MESH,
        )

    def copy_to(sem, src, dst, peer):
        return pltpu.make_async_remote_copy(
            src_ref=src, dst_ref=dst, send_sem=send_sem.at[sem], recv_sem=recv_sem.at[sem],
            device_id={"dap": peer}, device_id_type=pl.DeviceIdType.MESH,
        )

    def spread(which, src, dst, k=0, ds=None):
        def view(ref, at):
            return ref.at[at] if ds is None else ref.at[at, :, ds]

        for p in range(1, n):
            peer = lax.rem(me + p, n)
            copy_to(which * chunks + k, view(src, peer), view(dst, me), peer).start()
        if ds is None:
            dst[me] = src[me]
        else:
            dst[me, :, ds] = src[me, :, ds]

    def collect(which, src, dst, k=0, ds=None):
        def view(ref):
            return ref.at[pl.ds(0, n - 1)] if ds is None else ref.at[pl.ds(0, n - 1), :, ds]

        copy_to(which * chunks + k, view(src), view(dst), lax.rem(me + 1, n)).wait()

    def lanes_of(k):
        return pl.ds(pl.multiple_of(k * lc, lc), lc)

    def put(ref, ds, value):
        ref[:, :, ds] = value.reshape(n, per, lc).astype(BF16)

    def take(ref, ds):
        return ref[:, :, ds].astype(F32).reshape(c, lc)

    def to_slab(ref, slab, k, by_chunk=False):
        for s in range(n):
            block = ref[s, :, lanes_of(k)].astype(F32)
            row = (k * n + s) * crows if by_chunk else s * rows + k * crows
            for i in range(crows):
                part = block[:, i * res : (i + 1) * res]
                at = pl.ds(pl.multiple_of((row + i) * per, per), per)
                for t in range(tiles):
                    width = min(LANES, res - t * LANES)
                    slab[t, at, :width] = part[:, t * LANES : t * LANES + width]

    def matrix(slab, ch, first=0, count=res):
        at = pl.ds(first * per + ch, count, stride=per)
        parts = [slab[t, at, :] for t in range(tiles)]
        whole = parts[0] if tiles == 1 else jnp.concatenate(parts, axis=1)
        return whole[:, :res].astype(BF16)

    def keep(slab, ch, value, first=0):
        count = value.shape[0]
        pad = tiles * LANES - res
        if pad:
            value = jnp.concatenate([value, jnp.zeros((count, pad), F32)], axis=1)
        for t in range(tiles):
            at = pl.ds(first * per + ch, count, stride=per)
            slab[t, at, :] = value[:, t * LANES : (t + 1) * LANES]

    def from_slab(slab, ref, k, by_chunk=False):
        for s in range(n):
            row = (k * n + s) * crows if by_chunk else s * rows + k * crows
            parts = []
            for i in range(crows):
                at = pl.ds(pl.multiple_of((row + i) * per, per), per)
                for t in range(tiles):
                    width = min(LANES, res - t * LANES)
                    parts.append(slab[t, at, :width])
            ref[s, :, lanes_of(k)] = jnp.concatenate(parts, axis=1).astype(BF16)

    def early():
        return jnp.concatenate([acc_g[...], acc_f[...]], axis=1) * inv_count

    def hand_round(which, src, mine, dst):
        summed = jnp.sum(src[...].astype(F32), axis=0).astype(BF16)
        mine[...] = summed
        for p in range(1, n):
            copy_to(which * chunks, mine, dst.at[me], lax.rem(me + p, n)).start()
        dst[me] = summed

    def gathered(which, dst):
        block = dst.at[pl.ds(0, n - 1)]
        copy_to(which * chunks, block, block, lax.rem(me + 1, n)).wait()
        return dst[...].astype(F32).reshape(c, dst.shape[2])

    params = [embed[...], gain_on[...], gain_om[...], gain_in[...], gain_im[...]]
    cols[...] = jnp.concatenate(params + [jnp.zeros((2, c), F32)], axis=0).T
    here = lax.broadcasted_iota(jnp.int32, (rows, res), 1) == (
        lax.broadcasted_iota(jnp.int32, (rows, res), 0) + me * rows
    )
    row_mask = jnp.sum(jnp.where(here, residues[...], 0).astype(F32), axis=1, keepdims=True)
    row_chain = jnp.sum(jnp.where(here, chains[...], 0).astype(F32), axis=1, keepdims=True)
    both = row_mask * residues[...].astype(F32)
    same_chain = jnp.where(row_chain == chains[...].astype(F32), 1.0, 0.0)
    masks[0:1, :] = jnp.concatenate([both[i : i + 1] for i in range(rows)], axis=1)
    masks[1:2, :] = jnp.concatenate([same_chain[i : i + 1] for i in range(rows)], axis=1)
    emb0, emb1 = cols[:, 0:1], cols[:, 1:2]
    g_on, g_om, g_in, g_im = (cols[:, q : q + 1] for q in range(2, 6))

    def project(k):
        ds = lanes_of(k)
        same = masks[1:2, ds] > 0.5
        x = pair[ds, :].astype(F32).T + jnp.where(same, emb1, emb0)
        start[:, ds] = x
        hat, _ = norm_stats(x)
        nb = (hat * g_on).astype(BF16)
        normed[:, ds] = nb
        p = tn(out_proj[...], nb)
        pm = masks[0:1, ds]
        put(a_s, ds, pm * sigmoid(p[:c]) * p[c : 2 * c])
        put(b_s, ds, pm * sigmoid(p[2 * c : 3 * c]) * p[3 * c :])

    project(0)
    pl.semaphore_wait(barrier, n - 1)
    spread(B_OUT, b_s, b_r, 0, lanes_of(0))

    @pl.loop(1, chunks)
    def _(k):
        project(k)
        spread(B_OUT, b_s, b_r, k, lanes_of(k))

    @pl.loop(0, chunks)
    def _(k):
        spread(A_OUT, a_s, a_r, k, lanes_of(k))

    @pl.loop(0, chunks)
    def _(k):
        ds = lanes_of(k)
        gate[:, ds] = sigmoid(tn(out_gate[...], normed[:, ds]))
        cot_t[:, ds] = cot[ds, :].astype(F32).T

    @pl.loop(0, chunks)
    def _(k):
        collect(B_OUT, b_s, b_r, k, lanes_of(k))
        to_slab(b_r, slab_b, k)

    for ch in range(per):
        mat_b[ch] = matrix(slab_b, ch)

    group = n * crows

    @pl.loop(0, chunks)
    def _(k):
        ds = lanes_of(k)
        collect(A_OUT, a_s, a_r, k, ds)
        to_slab(a_r, slab_a, k, True)
        for ch in range(per):
            keep(slab_o, ch, nt(matrix(slab_a, ch, k * group, group), mat_b[ch]), k * group)
        from_slab(slab_o, x_s, k, True)
        spread(X_OUT, x_s, x_r, k, ds)

    @pl.loop(0, chunks)
    def _(k):
        ds = lanes_of(k)
        collect(X_OUT, x_s, x_r, k, ds)
        hat, _ = norm_stats(take(x_r, ds))
        y = (hat * g_om).astype(BF16)
        m = (start[:, ds] + gate[:, ds] * tn(out_final[...], y)).astype(BF16)
        mid[:, ds] = m
        hat, _ = norm_stats(m.astype(F32))
        nb = (hat * g_in).astype(BF16)
        normed[:, ds] = nb
        p = tn(in_proj[...], nb)
        in_p[:, ds] = p
        pm = masks[0:1, ds]
        put(a2_s, ds, pm * sigmoid(p[:c]) * p[c : 2 * c])
        put(b2_s, ds, pm * sigmoid(p[2 * c : 3 * c]) * p[3 * c :])
        spread(A_IN, a2_s, a2_r, k, ds)
        spread(B_IN, b2_s, b2_r, k, ds)

    @pl.loop(0, chunks)
    def _(k):
        ds = lanes_of(k)
        s = sigmoid(tn(in_gate[...], normed[:, ds]))
        logit_s[:, ds] = s
        v = (cot_t[:, ds] * s).astype(BF16)
        gv[:, ds] = v
        gy[:, ds] = nn(in_final[...], v)

    acc_p[...] = jnp.zeros_like(acc_p)
    acc_g[...] = jnp.zeros_like(acc_g)
    acc_f[...] = jnp.zeros_like(acc_f)
    acc_n[...] = jnp.zeros_like(acc_n)
    acc_m[...] = jnp.zeros_like(acc_m)

    @pl.loop(0, chunks)
    def _(k):
        collect(A_IN, a2_s, a2_r, k, lanes_of(k))
        to_slab(a2_r, slab_a, k)
        collect(B_IN, b2_s, b2_r, k, lanes_of(k))
        to_slab(b2_r, slab_b, k)

    for ch in range(per):
        a = matrix(slab_a, ch)
        b = matrix(slab_b, ch)
        mat_a[ch] = a
        mat_b[ch] = b
        keep(slab_o, ch, tn(a, b))

    @pl.loop(0, chunks)
    def _(k):
        from_slab(slab_o, x2_s, k)
        spread(X_IN, x2_s, x2_r, k, lanes_of(k))

    @pl.loop(0, chunks)
    def _(k):
        ds = lanes_of(k)
        collect(X_IN, x2_s, x2_r, k, ds)
        hat, inv = norm_stats(take(x2_r, ds))
        y = (hat * g_im).astype(BF16)
        value = tn(in_final[...], y)
        s = logit_s[:, ds]
        grad_l = (cot_t[:, ds] * value * s * (1.0 - s)).astype(BF16)
        gl[:, ds] = grad_l
        g = gy[:, ds]
        acc_m[...] += lane_sum(g * hat)
        put(gx_s, ds, norm_back(g, hat, inv, g_im))
        spread(G_X, gx_s, gx_r, k, ds)
        acc_f[...] += nt(y, gv[:, ds])

    @pl.loop(0, chunks)
    def _(k):
        ds = lanes_of(k)
        grad_l = gl[:, ds]
        acc_g[...] += nt(normed[:, ds], grad_l)
        gy[:, ds] = nn(in_gate[...], grad_l)

    h_s[...] = early().reshape(n, per, 2 * c).astype(BF16)
    spread(H_SUM, h_s, h_r)

    @pl.loop(0, chunks)
    def _(k):
        collect(G_X, gx_s, gx_r, k, lanes_of(k))
        to_slab(gx_r, slab_a, k)

    for ch in range(per):
        gx = matrix(slab_a, ch)
        mat_x[ch] = gx
        keep(slab_o, ch, nt(mat_b[ch], gx))

    @pl.loop(0, chunks)
    def _(k):
        from_slab(slab_o, ga_s, k)
        spread(G_A, ga_s, ga_r, k, lanes_of(k))

    for ch in range(per):
        keep(slab_p, ch, nn(mat_a[ch], mat_x[ch]))

    @pl.loop(0, chunks)
    def _(k):
        from_slab(slab_p, gb_s, k)
        spread(G_B, gb_s, gb_r, k, lanes_of(k))

    collect(H_SUM, h_s, h_r)
    hand_round(H_ALL, h_r, u_s, u_r)

    @pl.loop(0, chunks)
    def _(k):
        ds = lanes_of(k)
        collect(G_A, ga_s, ga_r, k, ds)
        collect(G_B, gb_s, gb_r, k, ds)
        pm = masks[0:1, ds]
        s0 = sigmoid(in_p[:c, ds])
        s2 = sigmoid(in_p[2 * c : 3 * c, ds])
        ga = take(ga_r, ds) * pm * s0
        gb = take(gb_r, ds) * pm * s2
        q0 = (ga * in_p[c : 2 * c, ds] * (1.0 - s0)).astype(BF16)
        q2 = (gb * in_p[3 * c :, ds] * (1.0 - s2)).astype(BF16)
        q = jnp.concatenate([q0, ga.astype(BF16), q2, gb.astype(BF16)], axis=0)
        in_q[:, ds] = q
        acc_p[...] += nt(normed[:, ds], q)

    g_s[...] = (acc_p[...] * inv_count).reshape(n, per, 4 * c).astype(BF16)
    spread(P_SUM, g_s, g_r)

    @pl.loop(0, chunks)
    def _(k):
        ds = lanes_of(k)
        g = nn(in_proj[...], in_q[:, ds]) + gy[:, ds]
        hat, inv = norm_stats(mid[:, ds].astype(F32))
        acc_n[...] += lane_sum(g * hat)
        z = cot_t[:, ds] + norm_back(g, hat, inv, g_in)
        grad_out[ds, :] = z.T.astype(BF16)

    lane = lax.broadcasted_iota(jnp.int32, (c, LANES), 1)
    gains = jnp.where(lane == 0, acc_n[...], jnp.where(lane == 1, acc_m[...], 0.0))
    w_s[...] = (gains * inv_count).T[:8]
    for p in range(1, n):
        copy_to(GAINS * chunks, w_s, w_r.at[me], lax.rem(me + p, n)).start()
    w_r[me] = w_s[...]
    collect(P_SUM, g_s, g_r)
    hand_round(P_ALL, g_r, t_s, t_r)
    both = gathered(H_ALL, u_r)
    gg_out[...] = both[:, :c]
    gf_out[...] = both[:, c:]
    block = w_r.at[pl.ds(0, n - 1)]
    copy_to(GAINS * chunks, block, block, lax.rem(me + 1, n)).wait()
    gain_sums = jnp.sum(w_r[...], axis=0)
    gn_out[...] = gain_sums[0:1]
    gm_out[...] = gain_sums[1:2]
    gp_out[...] = gathered(P_ALL, t_r)


def shards(n, pair, cotangent, residue_mask, chain_ids, chain_embed, out_norm_gain, out_proj,
           out_gate, out_mid_gain, out_final, in_norm_gain, in_proj, in_gate, in_mid_gain, in_final):
    rows, res, c = pair.shape
    total = rows * res
    per = c // n
    lc = res * min(
        q for q in range(1, rows + 1)
        if rows % q == 0 and q * res % LANES == 0 and (rows // q <= 3)
    )
    tiles = -(-res // LANES)
    def full(dtype):
        return pltpu.VMEM((c, total), dtype)

    swap = pltpu.VMEM((n, per, total), BF16)
    slab = pltpu.VMEM((tiles, res * per, LANES), F32)
    mats = pltpu.VMEM((per, res, res), BF16)
    wide = 4 * c
    scratch = [
        pltpu.VMEM((c, 8), F32), pltpu.VMEM((2, total), F32), pltpu.VMEM((4 * c, total), BF16), full(F32), full(BF16), full(F32),
        pltpu.VMEM((4 * c, total), F32), full(F32), full(BF16), full(F32), full(BF16), full(F32),
        full(BF16),
    ] + [swap] * 18 + [slab] * 4 + [mats] * 3 + [
        pltpu.VMEM((c, 4 * c), F32), pltpu.VMEM((c, c), F32), pltpu.VMEM((c, c), F32),
        pltpu.VMEM((c, 1), F32), pltpu.VMEM((c, 1), F32),
        pltpu.VMEM((n, per, wide), BF16), pltpu.VMEM((n, per, wide), BF16),
        pltpu.VMEM((per, wide), BF16), pltpu.VMEM((n, per, wide), BF16),
        pltpu.VMEM((n, per, 2 * c), BF16), pltpu.VMEM((n, per, 2 * c), BF16),
        pltpu.VMEM((per, 2 * c), BF16), pltpu.VMEM((n, per, 2 * c), BF16),
        pltpu.VMEM((8, c), F32), pltpu.VMEM((n, 8, c), F32),
        pltpu.SemaphoreType.DMA((14 * (total // lc),)), pltpu.SemaphoreType.DMA((14 * (total // lc),)),
    ]
    vmem = pl.BlockSpec(memory_space=pltpu.VMEM)
    grad, gp, gg, gf, gn, gm = pl.pallas_call(
        functools.partial(kernel, n, rows, res, lc),
        out_shape=(
            jax.ShapeDtypeStruct((total, c), BF16),
            jax.ShapeDtypeStruct((c, 4 * c), F32),
            jax.ShapeDtypeStruct((c, c), F32),
            jax.ShapeDtypeStruct((c, c), F32),
            jax.ShapeDtypeStruct((1, c), F32),
            jax.ShapeDtypeStruct((1, c), F32),
        ),
        in_specs=[vmem] * 15,
        out_specs=(vmem,) * 6,
        scratch_shapes=scratch,
        compiler_params=pltpu.CompilerParams(
            collective_id=0, has_side_effects=True, vmem_limit_bytes=60 * 1024 * 1024
        ),
    )(
        pair.reshape(total, c), cotangent.reshape(total, c),
        residue_mask.reshape(1, res), chain_ids.reshape(1, res), chain_embed,
        out_norm_gain.reshape(1, c), out_mid_gain.reshape(1, c),
        in_norm_gain.reshape(1, c), in_mid_gain.reshape(1, c),
        out_proj, out_gate, out_final, in_proj, in_gate, in_final,
    )
    return grad.reshape(rows, res, c), gp, gg, gf, gn.reshape(c), gm.reshape(c)


def solution(mesh):
    split = P("dap", "cplx", None)
    return jax.shard_map(
        functools.partial(shards, mesh.shape["dap"]),
        mesh=mesh,
        in_specs=(split, split, P("cplx"), P("cplx")) + (P(),) * 11,
        out_specs=(split, P("cplx", None), P("cplx", None), P("cplx", None), P("cplx"), P("cplx")),
        check_vma=False,
    )
```

profile of v0, /device:TPU:0, one launch (start us, length us, event | category | flops | bytes accessed | tf_op | source)
XLA Modules:
  0.0 88.4 jit_solution(5351483375776239998)
XLA Ops:
  0.6 82.5 %shard_map.190 = (bf16[1152,128]{1,0:T(8,128)(2,1)}, f32[128,512]{1,0:T(8,128)}, f32[128,128]{1,0:T(8,128)}, f32[128,128]{1,0:T(8,128)}, f32[1,128]{1,0:T(1,128)}, /*index=5*/f32[1,128]{1,0:T(1,128)}) custom-call(bf16[1152,128]{1,0:T(8,128)(2,1)} %bitcast.12, bf16[1152,128]{1,0:T(8,128)(2,1)} %bitcast.13, s32[1,96]{1,0:T(1,128)} %bitcast.14, ...), custom_call_target="tpu_custom_call" | custom-call | tf_op jit(solution)/shard_map/pallas_call | solution.py:412
  83.2 0.0 copy-start
  83.2 1.7 %copy.27 = bf16[12,96,128]{2,1,0:T(8,128)(2,1)} copy(bf16[12,96,128]{2,1,0:T(8,128)(2,1)} %bitcast.11) | data formatting | bytes 589824
  84.9 0.0 copy-done
  84.9 0.0 copy-start.2
  84.9 0.7 copy.28
  85.6 0.2 copy-done.2
  85.8 0.0 copy-start.1
  85.8 0.6 copy.29
  86.4 0.2 copy-done.1
  86.7 0.0 copy-start.4
  86.7 0.6 copy.30
  87.3 0.0 copy-done.4
  87.3 0.0 copy-start.3
  87.3 0.5 copy.31
  87.8 0.1 copy-done.3
  87.9 0.5 copy.32
Async XLA Ops:
  83.2 1.7 %copy-start = (f32[128,512]{1,0:T(8,128)S(1)}, f32[128,512]{1,0:T(8,128)}, u32[]{:S(2)}) copy-start(f32[128,512]{1,0:T(8,128)} %get-tuple-element.25) | copy-start | bytes 786436
  84.9 0.9 copy-start.2
  85.8 0.9 copy-start.1
  86.7 0.7 copy-start.4
  87.3 0.6 copy-start.3
where the time goes:
time: 88.7 us; the launch traced here: 88.4 us
  Pallas kernels  82.5 us (93%)
  local copies, waits for them, and re-layouts  5.21 us (6%)
    pallas_call x1, Pallas kernels, shards(): pl.pallas_call(functools.partial(kernel, n, rows, res, lc), out_shape=(ja...  82.5 us
    unnamed x16, local copies, waits for them, and re-layouts  5.21 us

commit v1 on v0

--- a/solution.py
+++ b/solution.py
@@ -377,6 +377,15 @@
     gp_out[...] = gathered(P_ALL, t_r)
 
 
+def write_out(*refs):
+    sems = refs[-1]
+    copies = [pltpu.make_async_copy(refs[q], refs[q + 6], sems.at[q]) for q in range(6)]
+    for copy in copies:
+        copy.start()
+    for copy in copies:
+        copy.wait()
+
+
 def shards(n, pair, cotangent, residue_mask, chain_ids, chain_embed, out_norm_gain, out_proj,
            out_gate, out_mid_gain, out_final, in_norm_gain, in_proj, in_gate, in_mid_gain, in_final):
     rows, res, c = pair.shape
@@ -409,21 +418,21 @@
         pltpu.SemaphoreType.DMA((14 * (total // lc),)), pltpu.SemaphoreType.DMA((14 * (total // lc),)),
     ]
     vmem = pl.BlockSpec(memory_space=pltpu.VMEM)
-    grad, gp, gg, gf, gn, gm = pl.pallas_call(
+    results = pl.pallas_call(
         functools.partial(kernel, n, rows, res, lc),
         out_shape=(
-            jax.ShapeDtypeStruct((total, c), BF16),
-            jax.ShapeDtypeStruct((c, 4 * c), F32),
-            jax.ShapeDtypeStruct((c, c), F32),
-            jax.ShapeDtypeStruct((c, c), F32),
-            jax.ShapeDtypeStruct((1, c), F32),
-            jax.ShapeDtypeStruct((1, c), F32),
+            pltpu.VMEM((total, c), BF16),
+            pltpu.VMEM((c, 4 * c), F32),
+            pltpu.VMEM((c, c), F32),
+            pltpu.VMEM((c, c), F32),
+            pltpu.VMEM((1, c), F32),
+            pltpu.VMEM((1, c), F32),
         ),
         in_specs=[vmem] * 15,
         out_specs=(vmem,) * 6,
         scratch_shapes=scratch,
         compiler_params=pltpu.CompilerParams(
-            collective_id=0, has_side_effects=True, vmem_limit_bytes=60 * 1024 * 1024
+            collective_id=0, has_side_effects=True, vmem_limit_bytes=56 * 1024 * 1024
         ),
     )(
         pair.reshape(total, c), cotangent.reshape(total, c),
@@ -432,6 +441,14 @@
         in_norm_gain.reshape(1, c), in_mid_gain.reshape(1, c),
         out_proj, out_gate, out_final, in_proj, in_gate, in_final,
     )
+    shapes = [((total, c), BF16), ((c, 4 * c), F32), ((c, c), F32), ((c, c), F32), ((1, c), F32), ((1, c), F32)]
+    grad, gp, gg, gf, gn, gm = pl.pallas_call(
+        write_out,
+        out_shape=[jax.ShapeDtypeStruct(*shape) for shape in shapes],
+        in_specs=[pl.BlockSpec(memory_space=pltpu.VMEM)] * 6,
+        out_specs=[pl.BlockSpec(memory_space=pl.ANY)] * 6,
+        scratch_shapes=[pltpu.SemaphoreType.DMA((6,))],
+    )(*[pltpu.with_memory_space_constraint(r, pltpu.VMEM) for r in results])
     return grad.reshape(rows, res, c), gp, gg, gf, gn.reshape(c), gm.reshape(c)
 
 

time: 88.7 us -> 83.4 us (0.940)
  local copies, waits for them, and re-layouts: 5.21 us -> 0 us
    unnamed x16 -> x0, local copies, waits for them, and re-layouts: 5.21 us -> none
    pallas_call x1 -> x2, Pallas kernels: 82.5 us -> 82.6 us  [the longest x1 81.7 us: shards(): pl.pallas_call(functools.partial(kernel, n, rows, res, lc), out_shape=(pl...]
where the time goes in v1:
time: 83.4 us; the launch traced here: 83.2 us
  Pallas kernels  82.6 us (99%)
    pallas_call x1, Pallas kernels, shards(): pl.pallas_call(functools.partial(kernel, n, rows, res, lc), out_shape=(pl...  81.7 us

profile of v1, /device:TPU:0, one launch (start us, length us, event | category | flops | bytes accessed | tf_op | source)
XLA Modules:
  0.0 83.2 jit_solution(584701654292694877)
XLA Ops:
  0.6 81.7 %shard_map.190 = (bf16[1152,128]{1,0:T(8,128)(2,1)S(1)}, f32[128,512]{1,0:T(8,128)S(1)}, f32[128,128]{1,0:T(8,128)S(1)}, f32[128,128]{1,0:T(8,128)S(1)}, f32[1,128]{1,0:T(1,128)S(1)}, /*index=5*/f32[1,128]{1,0:T(1,128)S(1)}) custom-call(bf16[1152,128]{1,0:T(8,128)(2,1)} %bitcast.11, bf16[1152,128]{1,0:T(8,128)(2,1)} %bitcast.12, s32[1,96]{1,0:T(1,128)} %bitcast.13, ...), custom_call_target="tpu_custom_call" | custom-call | tf_op jit(solution)/shard_map/pallas_call | solution.py:421
  82.3 0.9 %shard_map.191 = (bf16[1152,128]{1,0:T(8,128)(2,1)}, f32[128,512]{1,0:T(8,128)}, f32[128,128]{1,0:T(8,128)}, f32[128,128]{1,0:T(8,128)}, f32[1,128]{1,0:T(1,128)}, /*index=5*/f32[1,128]{1,0:T(1,128)}) custom-call(bf16[1152,128]{1,0:T(8,128)(2,1)S(1)} %get-tuple-element.18.refs_0_, f32[128,512]{1,0:T(8,128)S(1)} %get-tuple-element.19.refs_1_, ...), custom_call_target="tpu_custom_call" | custom-call | tf_op jit(solution)/shard_map/pallas_call | solution.py:445

commit v2 on v1

--- a/solution.py
+++ b/solution.py
@@ -10,6 +10,7 @@
 F32 = jnp.float32
 BF16 = jnp.bfloat16
 LANES = 128
+PAD = 8
 A_OUT, B_OUT, X_OUT, A_IN, B_IN, X_IN, G_X, G_A, G_B, P_SUM, P_ALL, H_SUM, H_ALL, GAINS = range(14)
 
 
@@ -47,20 +48,26 @@
 
 
 def kernel(
-    n, rows, res, lc,
+    n, rows, res, lc, pitch,
     pair, cot, residues, chains, embed, gain_on, gain_om, gain_in, gain_im, out_proj, out_gate, out_final, in_proj, in_gate, in_final,
     grad_out, gp_out, gg_out, gf_out, gn_out, gm_out,
     cols, masks, in_q, start, normed, gate, in_p, cot_t, mid, logit_s, gv, gy, gl,
     a_s, b_s, x_s, a_r, b_r, x_r,
     a2_s, b2_s, x2_s, a2_r, b2_r, x2_r,
     gx_s, gx_r, ga_s, gb_s, ga_r, gb_r,
-    slab_a, slab_b, slab_o, slab_p, mat_a, mat_b, mat_x,
+    slab_a, slab_b, slab_o, mat_a, mat_b,
     acc_p, acc_g, acc_f, acc_n, acc_m, g_s, g_r, t_s, t_r, h_s, h_r, u_s, u_r, w_s, w_r,
     send_sem, recv_sem,
 ):
     me = lax.axis_index("dap")
     c = start.shape[0]
     per = c // n
+    m = n // 2
+    parts, hs = a_s.shape[1], a_s.shape[2]
+    mine = lax.rem(me, m)
+    base = me - mine
+    away = m - base
+    half = m * rows
     total = rows * res
     chunks = total // lc
     crows = lc // res
@@ -80,83 +87,103 @@
             device_id={"dap": peer}, device_id_type=pl.DeviceIdType.MESH,
         )
 
-    def spread(which, src, dst, k=0, ds=None):
-        def view(ref, at):
-            return ref.at[at] if ds is None else ref.at[at, :, ds]
-
+    def flag(which, k=0, h=0):
+        return (which * parts + h) * chunks + k
+
+    def near(which, src, dst, h, k):
+        ds = lanes_of(k)
+        for p in range(1, m):
+            slot = lax.rem(mine + p, m)
+            copy_to(flag(which, k, h), src.at[slot, h, :, ds], dst.at[mine, h, :, ds], base + slot).start()
+        dst[mine, h, :, ds] = src[mine, h, :, ds]
+
+    def far(which, src, dst, h, k, by_peer=False):
+        ds = lanes_of(k)
+        for p in range(m):
+            slot = lax.rem(mine + p, m)
+            peer = away + slot
+            copy_to(flag(which, k, h), src.at[peer if by_peer else slot, h, :, ds], dst.at[me, h, :, ds], peer).start()
+        for p in range(1, m):
+            slot = lax.rem(mine + p, m)
+            peer = base + slot
+            copy_to(flag(which, k, h), src.at[peer if by_peer else slot, h, :, ds], dst.at[me, h, :, ds], peer).start()
+        dst[me, h, :, ds] = src[me if by_peer else mine, h, :, ds]
+
+    def collect(which, dst, h, k):
+        block = dst.at[pl.ds(0, dst.shape[0] - 1), h, :, lanes_of(k)]
+        copy_to(flag(which, k, h), block, block, lax.rem(me + 1, n)).wait()
+
+    def spread(which, src, dst):
         for p in range(1, n):
             peer = lax.rem(me + p, n)
-            copy_to(which * chunks + k, view(src, peer), view(dst, me), peer).start()
-        if ds is None:
-            dst[me] = src[me]
-        else:
-            dst[me, :, ds] = src[me, :, ds]
-
-    def collect(which, src, dst, k=0, ds=None):
-        def view(ref):
-            return ref.at[pl.ds(0, n - 1)] if ds is None else ref.at[pl.ds(0, n - 1), :, ds]
-
-        copy_to(which * chunks + k, view(src), view(dst), lax.rem(me + 1, n)).wait()
+            copy_to(flag(which), src.at[peer], dst.at[me], peer).start()
+        dst[me] = src[me]
+
+    def gather(which, dst):
+        block = dst.at[pl.ds(0, n - 1)]
+        copy_to(flag(which), block, block, lax.rem(me + 1, n)).wait()
 
     def lanes_of(k):
         return pl.ds(pl.multiple_of(k * lc, lc), lc)
 
     def put(ref, ds, value):
-        ref[:, :, ds] = value.reshape(n, per, lc).astype(BF16)
+        ref[:, :, :, ds] = value.reshape(m, parts, hs, lc).astype(BF16)
 
     def take(ref, ds):
-        return ref[:, :, ds].astype(F32).reshape(c, lc)
-
-    def to_slab(ref, slab, k, by_chunk=False):
-        for s in range(n):
-            block = ref[s, :, lanes_of(k)].astype(F32)
-            row = (k * n + s) * crows if by_chunk else s * rows + k * crows
+        return ref[:, :, :, ds].astype(F32).reshape(c, lc)
+
+    def take_sum(ref, ds):
+        both = ref[pl.ds(0, m), :, :, ds].astype(F32) + ref[pl.ds(m, m), :, :, ds].astype(F32)
+        return both.reshape(c, lc)
+
+    def to_slab(ref, slab, h, k):
+        for s in range(ref.shape[0]):
+            block = ref[s, h, :, lanes_of(k)].astype(F32)
+            row = s * rows + k * crows
             for i in range(crows):
                 part = block[:, i * res : (i + 1) * res]
-                at = pl.ds(pl.multiple_of((row + i) * per, per), per)
+                at = pl.ds(pl.multiple_of((row + i) * pitch + h * hs, 8), hs)
                 for t in range(tiles):
                     width = min(LANES, res - t * LANES)
                     slab[t, at, :width] = part[:, t * LANES : t * LANES + width]
 
-    def matrix(slab, ch, first=0, count=res):
-        at = pl.ds(first * per + ch, count, stride=per)
-        parts = [slab[t, at, :] for t in range(tiles)]
-        whole = parts[0] if tiles == 1 else jnp.concatenate(parts, axis=1)
+    def matrix(slab, ch, count):
+        at = pl.ds(ch, count, stride=pitch)
+        pieces = [slab[t, at, :] for t in range(tiles)]
+        whole = pieces[0] if tiles == 1 else jnp.concatenate(pieces, axis=1)
         return whole[:, :res].astype(BF16)
 
-    def keep(slab, ch, value, first=0):
+    def keep(slab, ch, value):
         count = value.shape[0]
         pad = tiles * LANES - res
         if pad:
             value = jnp.concatenate([value, jnp.zeros((count, pad), F32)], axis=1)
         for t in range(tiles):
-            at = pl.ds(first * per + ch, count, stride=per)
-            slab[t, at, :] = value[:, t * LANES : (t + 1) * LANES]
-
-    def from_slab(slab, ref, k, by_chunk=False):
-        for s in range(n):
-            row = (k * n + s) * crows if by_chunk else s * rows + k * crows
-            parts = []
+            slab[t, pl.ds(ch, count, stride=pitch), :] = value[:, t * LANES : (t + 1) * LANES]
+
+    def from_slab(slab, ref, h, k):
+        for s in range(ref.shape[0]):
+            row = s * rows + k * crows
+            pieces = []
             for i in range(crows):
-                at = pl.ds(pl.multiple_of((row + i) * per, per), per)
+                at = pl.ds(pl.multiple_of((row + i) * pitch + h * hs, 8), hs)
                 for t in range(tiles):
                     width = min(LANES, res - t * LANES)
-                    parts.append(slab[t, at, :width])
-            ref[s, :, lanes_of(k)] = jnp.concatenate(parts, axis=1).astype(BF16)
+                    pieces.append(slab[t, at, :width])
+            ref[s, h, :, lanes_of(k)] = jnp.concatenate(pieces, axis=1).astype(BF16)
 
     def early():
         return jnp.concatenate([acc_g[...], acc_f[...]], axis=1) * inv_count
 
-    def hand_round(which, src, mine, dst):
+    def hand_round(which, src, own, dst):
         summed = jnp.sum(src[...].astype(F32), axis=0).astype(BF16)
-        mine[...] = summed
+        own[...] = summed
         for p in range(1, n):
-            copy_to(which * chunks, mine, dst.at[me], lax.rem(me + p, n)).start()
+            copy_to(flag(which), own, dst.at[me], lax.rem(me + p, n)).start()
         dst[me] = summed
 
     def gathered(which, dst):
-        block = dst.at[pl.ds(0, n - 1)]
-        copy_to(which * chunks, block, block, lax.rem(me + 1, n)).wait()
+        gather(which, dst)
         return dst[...].astype(F32).reshape(c, dst.shape[2])
 
     params = [embed[...], gain_on[...], gain_om[...], gain_in[...], gain_im[...]]
@@ -186,18 +213,9 @@
         put(a_s, ds, pm * sigmoid(p[:c]) * p[c : 2 * c])
         put(b_s, ds, pm * sigmoid(p[2 * c : 3 * c]) * p[3 * c :])
 
-    project(0)
-    pl.semaphore_wait(barrier, n - 1)
-    spread(B_OUT, b_s, b_r, 0, lanes_of(0))
-
-    @pl.loop(1, chunks)
+    @pl.loop(0, chunks)
     def _(k):
         project(k)
-        spread(B_OUT, b_s, b_r, k, lanes_of(k))
-
-    @pl.loop(0, chunks)
-    def _(k):
-        spread(A_OUT, a_s, a_r, k, lanes_of(k))
 
     @pl.loop(0, chunks)
     def _(k):
@@ -205,35 +223,39 @@
         gate[:, ds] = sigmoid(tn(out_gate[...], normed[:, ds]))
         cot_t[:, ds] = cot[ds, :].astype(F32).T
 
-    @pl.loop(0, chunks)
-    def _(k):
-        collect(B_OUT, b_s, b_r, k, lanes_of(k))
-        to_slab(b_r, slab_b, k)
-
-    for ch in range(per):
-        mat_b[ch] = matrix(slab_b, ch)
-
-    group = n * crows
-
-    @pl.loop(0, chunks)
-    def _(k):
-        ds = lanes_of(k)
-        collect(A_OUT, a_s, a_r, k, ds)
-        to_slab(a_r, slab_a, k, True)
-        for ch in range(per):
-            keep(slab_o, ch, nt(matrix(slab_a, ch, k * group, group), mat_b[ch]), k * group)
-        from_slab(slab_o, x_s, k, True)
-        spread(X_OUT, x_s, x_r, k, ds)
-
-    @pl.loop(0, chunks)
-    def _(k):
-        ds = lanes_of(k)
-        collect(X_OUT, x_s, x_r, k, ds)
+    pl.semaphore_wait(barrier, n - 1)
+    for h in range(parts):
+        @pl.loop(0, chunks)
+        def _(k):
+            near(A_OUT, a_s, a_r, h, k)
+            far(B_OUT, b_s, b_r, h, k)
+
+    for h in range(parts):
+        @pl.loop(0, chunks)
+        def _(k):
+            collect(A_OUT, a_r, h, k)
+            to_slab(a_r, slab_a, h, k)
+            collect(B_OUT, b_r, h, k)
+            to_slab(b_r, slab_b, h, k)
+
+        for ch in range(h * hs, (h + 1) * hs):
+            keep(slab_o, ch, nt(matrix(slab_a, ch, half), matrix(slab_b, ch, res)))
+
+        @pl.loop(0, chunks)
+        def _(k):
+            from_slab(slab_o, x_s, h, k)
+            near(X_OUT, x_s, x_r, h, k)
+
+    @pl.loop(0, chunks)
+    def _(k):
+        ds = lanes_of(k)
+        for h in range(parts):
+            collect(X_OUT, x_r, h, k)
         hat, _ = norm_stats(take(x_r, ds))
         y = (hat * g_om).astype(BF16)
-        m = (start[:, ds] + gate[:, ds] * tn(out_final[...], y)).astype(BF16)
-        mid[:, ds] = m
-        hat, _ = norm_stats(m.astype(F32))
+        v = (start[:, ds] + gate[:, ds] * tn(out_final[...], y)).astype(BF16)
+        mid[:, ds] = v
+        hat, _ = norm_stats(v.astype(F32))
         nb = (hat * g_in).astype(BF16)
         normed[:, ds] = nb
         p = tn(in_proj[...], nb)
@@ -241,8 +263,14 @@
         pm = masks[0:1, ds]
         put(a2_s, ds, pm * sigmoid(p[:c]) * p[c : 2 * c])
         put(b2_s, ds, pm * sigmoid(p[2 * c : 3 * c]) * p[3 * c :])
-        spread(A_IN, a2_s, a2_r, k, ds)
-        spread(B_IN, b2_s, b2_r, k, ds)
+        near(A_IN, a2_s, a2_r, 0, k)
+        near(B_IN, b2_s, b2_r, 0, k)
+
+    for h in range(1, parts):
+        @pl.loop(0, chunks)
+        def _(k):
+            near(A_IN, a2_s, a2_r, h, k)
+            near(B_IN, b2_s, b2_r, h, k)
 
     @pl.loop(0, chunks)
     def _(k):
@@ -259,30 +287,32 @@
     acc_n[...] = jnp.zeros_like(acc_n)
     acc_m[...] = jnp.zeros_like(acc_m)
 
-    @pl.loop(0, chunks)
-    def _(k):
-        collect(A_IN, a2_s, a2_r, k, lanes_of(k))
-        to_slab(a2_r, slab_a, k)
-        collect(B_IN, b2_s, b2_r, k, lanes_of(k))
-        to_slab(b2_r, slab_b, k)
-
-    for ch in range(per):
-        a = matrix(slab_a, ch)
-        b = matrix(slab_b, ch)
-        mat_a[ch] = a
-        mat_b[ch] = b
-        keep(slab_o, ch, tn(a, b))
-
-    @pl.loop(0, chunks)
-    def _(k):
-        from_slab(slab_o, x2_s, k)
-        spread(X_IN, x2_s, x2_r, k, lanes_of(k))
-
-    @pl.loop(0, chunks)
-    def _(k):
-        ds = lanes_of(k)
-        collect(X_IN, x2_s, x2_r, k, ds)
-        hat, inv = norm_stats(take(x2_r, ds))
+    for h in range(parts):
+        @pl.loop(0, chunks)
+        def _(k):
+            collect(A_IN, a2_r, h, k)
+            to_slab(a2_r, slab_a, h, k)
+            collect(B_IN, b2_r, h, k)
+            to_slab(b2_r, slab_b, h, k)
+
+        for ch in range(h * hs, (h + 1) * hs):
+            a = matrix(slab_a, ch, half)
+            b = matrix(slab_b, ch, half)
+            mat_a[ch] = a
+            mat_b[ch] = b
+            keep(slab_o, ch, tn(a, b))
+
+        @pl.loop(0, chunks)
+        def _(k):
+            from_slab(slab_o, x2_s, h, k)
+            far(X_IN, x2_s, x2_r, h, k, True)
+
+    @pl.loop(0, chunks)
+    def _(k):
+        ds = lanes_of(k)
+        for h in range(parts):
+            collect(X_IN, x2_r, h, k)
+        hat, inv = norm_stats(take_sum(x2_r, ds))
         y = (hat * g_im).astype(BF16)
         value = tn(in_final[...], y)
         s = logit_s[:, ds]
@@ -291,8 +321,13 @@
         g = gy[:, ds]
         acc_m[...] += lane_sum(g * hat)
         put(gx_s, ds, norm_back(g, hat, inv, g_im))
-        spread(G_X, gx_s, gx_r, k, ds)
+        far(G_X, gx_s, gx_r, 0, k)
         acc_f[...] += nt(y, gv[:, ds])
+
+    for h in range(1, parts):
+        @pl.loop(0, chunks)
+        def _(k):
+            far(G_X, gx_s, gx_r, h, k)
 
     @pl.loop(0, chunks)
     def _(k):
@@ -304,37 +339,33 @@
     h_s[...] = early().reshape(n, per, 2 * c).astype(BF16)
     spread(H_SUM, h_s, h_r)
 
-    @pl.loop(0, chunks)
-    def _(k):
-        collect(G_X, gx_s, gx_r, k, lanes_of(k))
-        to_slab(gx_r, slab_a, k)
-
-    for ch in range(per):
-        gx = matrix(slab_a, ch)
-        mat_x[ch] = gx
-        keep(slab_o, ch, nt(mat_b[ch], gx))
-
-    @pl.loop(0, chunks)
-    def _(k):
-        from_slab(slab_o, ga_s, k)
-        spread(G_A, ga_s, ga_r, k, lanes_of(k))
-
-    for ch in range(per):
-        keep(slab_p, ch, nn(mat_a[ch], mat_x[ch]))
-
-    @pl.loop(0, chunks)
-    def _(k):
-        from_slab(slab_p, gb_s, k)
-        spread(G_B, gb_s, gb_r, k, lanes_of(k))
-
-    collect(H_SUM, h_s, h_r)
+    for h in range(parts):
+        @pl.loop(0, chunks)
+        def _(k):
+            collect(G_X, gx_r, h, k)
+            to_slab(gx_r, slab_a, h, k)
+
+        for ch in range(h * hs, (h + 1) * hs):
+            gx = matrix(slab_a, ch, res)
+            keep(slab_o, ch, nt(mat_b[ch], gx))
+            keep(slab_b, ch, nn(mat_a[ch], gx))
+
+        @pl.loop(0, chunks)
+        def _(k):
+            from_slab(slab_o, ga_s, h, k)
+            near(G_A, ga_s, ga_r, h, k)
+            from_slab(slab_b, gb_s, h, k)
+            near(G_B, gb_s, gb_r, h, k)
+
+    gather(H_SUM, h_r)
     hand_round(H_ALL, h_r, u_s, u_r)
 
     @pl.loop(0, chunks)
     def _(k):
         ds = lanes_of(k)
-        collect(G_A, ga_s, ga_r, k, ds)
-        collect(G_B, gb_s, gb_r, k, ds)
+        for h in range(parts):
+            collect(G_A, ga_r, h, k)
+            collect(G_B, gb_r, h, k)
         pm = masks[0:1, ds]
         s0 = sigmoid(in_p[:c, ds])
         s2 = sigmoid(in_p[2 * c : 3 * c, ds])
@@ -362,15 +393,14 @@
     gains = jnp.where(lane == 0, acc_n[...], jnp.where(lane == 1, acc_m[...], 0.0))
     w_s[...] = (gains * inv_count).T[:8]
     for p in range(1, n):
-        copy_to(GAINS * chunks, w_s, w_r.at[me], lax.rem(me + p, n)).start()
+        copy_to(flag(GAINS), w_s, w_r.at[me], lax.rem(me + p, n)).start()
     w_r[me] = w_s[...]
-    collect(P_SUM, g_s, g_r)
+    gather(P_SUM, g_r)
     hand_round(P_ALL, g_r, t_s, t_r)
     both = gathered(H_ALL, u_r)
     gg_out[...] = both[:, :c]
     gf_out[...] = both[:, c:]
-    block = w_r.at[pl.ds(0, n - 1)]
-    copy_to(GAINS * chunks, block, block, lax.rem(me + 1, n)).wait()
+    gather(GAINS, w_r)
     gain_sums = jnp.sum(w_r[...], axis=0)
     gn_out[...] = gain_sums[0:1]
     gm_out[...] = gain_sums[1:2]
@@ -399,15 +429,24 @@
     def full(dtype):
         return pltpu.VMEM((c, total), dtype)
 
-    swap = pltpu.VMEM((n, per, total), BF16)
-    slab = pltpu.VMEM((tiles, res * per, LANES), F32)
-    mats = pltpu.VMEM((per, res, res), BF16)
+    m = n // 2
+    hc = c // m
+    parts = 2 if hc % 32 == 0 else 1
+    pitch = hc + PAD
+    swap = pltpu.VMEM((m, parts, hc // parts, total), BF16)
+    whole = pltpu.VMEM((n, parts, hc // parts, total), BF16)
+    slab = pltpu.VMEM((tiles, res * pitch, LANES), F32)
+    mats = pltpu.VMEM((hc, m * rows, res), BF16)
     wide = 4 * c
     scratch = [
         pltpu.VMEM((c, 8), F32), pltpu.VMEM((2, total), F32), pltpu.VMEM((4 * c, total), BF16), full(F32), full(BF16), full(F32),
         pltpu.VMEM((4 * c, total), F32), full(F32), full(BF16), full(F32), full(BF16), full(F32),
         full(BF16),
-    ] + [swap] * 18 + [slab] * 4 + [mats] * 3 + [
+    ] + [
+        swap, swap, swap, swap, whole, swap,
+        swap, swap, whole, swap, swap, whole,
+        swap, whole, swap, swap, swap, swap,
+    ] + [slab] * 3 + [mats] * 2 + [
         pltpu.VMEM((c, 4 * c), F32), pltpu.VMEM((c, c), F32), pltpu.VMEM((c, c), F32),
         pltpu.VMEM((c, 1), F32), pltpu.VMEM((c, 1), F32),
         pltpu.VMEM((n, per, wide), BF16), pltpu.VMEM((n, per, wide), BF16),
@@ -415,11 +454,11 @@
         pltpu.VMEM((n, per, 2 * c), BF16), pltpu.VMEM((n, per, 2 * c), BF16),
         pltpu.VMEM((per, 2 * c), BF16), pltpu.VMEM((n, per, 2 * c), BF16),
         pltpu.VMEM((8, c), F32), pltpu.VMEM((n, 8, c), F32),
-        pltpu.SemaphoreType.DMA((14 * (total // lc),)), pltpu.SemaphoreType.DMA((14 * (total // lc),)),
+        pltpu.SemaphoreType.DMA((14 * parts * (total // lc),)), pltpu.SemaphoreType.DMA((14 * parts * (total // lc),)),
     ]
     vmem = pl.BlockSpec(memory_space=pltpu.VMEM)
     results = pl.pallas_call(
-        functools.partial(kernel, n, rows, res, lc),
+        functools.partial(kernel, n, rows, res, lc, pitch),
         out_shape=(
             pltpu.VMEM((total, c), BF16),
             pltpu.VMEM((c, 4 * c), F32),

time: 83.4 us -> 78.6 us (0.942)
  Pallas kernels: 82.6 us -> 77.8 us
    pallas_call x1, Pallas kernels: 81.7 us -> 76.9 us  [shards(): pl.pallas_call(functools.partial(kernel, n, rows, res, lc, pitch), out_sh...]
where the time goes in v2:
time: 78.6 us; the launch traced here: 78.4 us
  Pallas kernels  77.8 us (99%)
    pallas_call x1, Pallas kernels, shards(): pl.pallas_call(functools.partial(kernel, n, rows, res, lc, pitch), out_sh...  76.9 us

profile of v2, /device:TPU:0, one launch (start us, length us, event | category | flops | bytes accessed | tf_op | source)
XLA Modules:
  0.0 78.4 jit_solution(296097865666088012)
XLA Ops:
  0.6 76.9 %shard_map.190 = (bf16[1152,128]{1,0:T(8,128)(2,1)S(1)}, f32[128,512]{1,0:T(8,128)S(1)}, f32[128,128]{1,0:T(8,128)S(1)}, f32[128,128]{1,0:T(8,128)S(1)}, f32[1,128]{1,0:T(1,128)S(1)}, /*index=5*/f32[1,128]{1,0:T(1,128)S(1)}) custom-call(bf16[1152,128]{1,0:T(8,128)(2,1)} %bitcast.11, bf16[1152,128]{1,0:T(8,128)(2,1)} %bitcast.12, s32[1,96]{1,0:T(1,128)} %bitcast.13, ...), custom_call_target="tpu_custom_call" | custom-call | tf_op jit(solution)/shard_map/pallas_call | solution.py:460
  77.5 0.9 %shard_map.191 = (bf16[1152,128]{1,0:T(8,128)(2,1)}, f32[128,512]{1,0:T(8,128)}, f32[128,128]{1,0:T(8,128)}, f32[128,128]{1,0:T(8,128)}, f32[1,128]{1,0:T(1,128)}, /*index=5*/f32[1,128]{1,0:T(1,128)}) custom-call(bf16[1152,128]{1,0:T(8,128)(2,1)S(1)} %get-tuple-element.18.refs_0_, f32[128,512]{1,0:T(8,128)S(1)} %get-tuple-element.19.refs_1_, ...), custom_call_target="tpu_custom_call" | custom-call | tf_op jit(solution)/shard_map/pallas_call | solution.py:484

commit v3 on v2

v3 whole, which is shorter than its diff:
```python
import functools

import jax
import jax.numpy as jnp
from jax import lax
from jax.experimental import pallas as pl
from jax.experimental.pallas import tpu as pltpu
from jax.sharding import PartitionSpec as P

F32 = jnp.float32
BF16 = jnp.bfloat16
LANES = 128
PAD = 8
ALL = (slice(None),)
A_OUT, B_OUT, X_OUT, AB_H, X_H, G_H, D_H, AB_E, X_E, G_E, D_E, GAINS, P_SUM, P_ALL, T_NEAR, T_OVER, T_BACK = range(17)


def tn(w, x):
    return lax.dot_general(w, x, (((0,), (0,)), ((), ())), preferred_element_type=F32)


def nn(w, x):
    return jnp.dot(w, x, preferred_element_type=F32)


def nt(w, x):
    return lax.dot_general(w, x, (((1,), (1,)), ((), ())), preferred_element_type=F32)


def sigmoid(v):
    return 1.0 / (1.0 + jnp.exp(-v))


def norm_stats(v):
    centred = v - jnp.mean(v, axis=0, keepdims=True)
    inv = lax.rsqrt(jnp.mean(centred * centred, axis=0, keepdims=True) + 1e-05)
    return centred * inv, inv


def norm_back(grad, hat, inv, gain):
    scaled = grad * gain
    m1 = jnp.mean(scaled, axis=0, keepdims=True)
    m2 = jnp.mean(scaled * hat, axis=0, keepdims=True)
    return inv * (scaled - m1 - hat * m2)


def lane_sum(v):
    return jnp.sum(v, axis=1, keepdims=True)


def receive_slots(parts, chunks):
    counts = [parts, parts, parts - 1 + chunks] + [chunks] * 8 + [1, 1, 1, 2, 2, 2]
    return [sum(counts[:q]) for q in range(len(counts) + 1)]


def kernel(
    n, rows, res, lc, pitch, every,
    pair_h, cot_h, residues_h, chains_h, embed_h, gain_on_h, gain_om_h, gain_in_h, gain_im_h,
    out_proj_h, out_gate_h, out_final_h, in_proj_h, in_gate_h, in_final_h,
    grad_out, gp_out, gg_out, gf_out, gn_out, gm_out,
    pair, cot, residues, chains, embed, gain_on, gain_om, gain_in, gain_im,
    out_proj, out_gate, out_final, in_proj, in_gate, in_final,
    cols, masks, in_q, start, normed, gate, in_p, cot_t, mid, logit_s, gv, gy, gl,
    a_s, b_s, x_s, a_r, b_r, x_r,
    abh_s, abh_r, xh_s, xh_r, gh_s, gh_r, dh_s, dh_r,
    abe_s, abe_r, xe_s, xe_r, ge_s, ge_r, de_s, de_r,
    slab_a, slab_b, slab_o, mat_a, mat_b, mate_a, mate_b,
    acc_p, acc_g, acc_f, acc_n, acc_m, g_s, g_r, t_s, t_r,
    h_s, h_r, h_own, h_other, h_mean, h_back, f_s, f_r, f_own, f_other, f_mean, f_back, w_s, w_r,
    in_sem, send_sem, recv_sem,
):
    me = lax.axis_index("dap")
    c = start.shape[0]
    per = c // n
    m = n // 2
    parts, hs = a_s.shape[0], a_s.shape[2]
    mine = lax.rem(me, m)
    base = me - mine
    away = m - base
    half = m * rows
    total = rows * res
    chunks = total // lc
    crows = lc // res
    tiles = -(-res // LANES)
    inv_count = 1.0 / res
    we, wh = every // n, (c - every) // m
    groups = ([(0, every)] if every else []) + [(every, c - every)]

    barrier = pltpu.get_barrier_semaphore()
    for p in range(1, n):
        pl.semaphore_signal(
            barrier, inc=1, device_id={"dap": lax.rem(me + p, n)},
            device_id_type=pl.DeviceIdType.MESH,
        )
    sources = [
        pair_h, embed_h, gain_on_h, gain_om_h, gain_in_h, gain_im_h, residues_h, chains_h, out_proj_h,
        out_gate_h, cot_h, out_final_h, in_proj_h, in_gate_h, in_final_h,
    ]
    targets = [
        pair, embed, gain_on, gain_om, gain_in, gain_im, residues, chains, out_proj,
        out_gate, cot, out_final, in_proj, in_gate, in_final,
    ]
    loads = [pltpu.make_async_copy(a, b, in_sem.at[q]) for q, (a, b) in enumerate(zip(sources, targets))]
    for load in loads:
        load.start()

    first_of = receive_slots(parts, chunks)

    def copy_to(which, k, src, dst, peer):
        return pltpu.make_async_remote_copy(
            src_ref=src, dst_ref=dst, send_sem=send_sem.at[which], recv_sem=recv_sem.at[first_of[which] + k],
            device_id={"dap": peer}, device_id_type=pl.DeviceIdType.MESH,
        )

    def lanes_of(k):
        return pl.ds(pl.multiple_of(k * lc, lc), lc)

    def near(which, key, src, dst, lead, ds):
        for p in range(1, m):
            slot = lax.rem(mine + p, m)
            copy_to(which, key, src.at[(*lead, slot, slice(None), ds)], dst.at[(*lead, mine, slice(None), ds)], base + slot).start()
        dst[(*lead, mine, slice(None), ds)] = src[(*lead, mine, slice(None), ds)]

    def far(which, key, src, dst, lead, ds, by_peer=False):
        for first, other in ((0, True), (1, False)):
            for p in range(first, m):
                slot = lax.rem(mine + p, m)
                peer = (away if other else base) + slot
                at = peer if by_peer else slot
                copy_to(which, key, src.at[(*lead, at, slice(None), ds)], dst.at[(*lead, me, slice(None), ds)], peer).start()
        dst[(*lead, me, slice(None), ds)] = src[(*lead, me if by_peer else mine, slice(None), ds)]

    def across(which, key, src, dst, lead, ds, other):
        for p in range(0 if other else 1, m):
            peer = (away if other else base) + lax.rem(mine + p, m)
            copy_to(which, key, src.at[(*lead, peer, slice(None), ds)], dst.at[(*lead, me, slice(None), ds)], peer).start()
        if not other:
            dst[(*lead, me, slice(None), ds)] = src[(*lead, me, slice(None), ds)]

    def arrived(which, key, block):
        copy_to(which, key, block, block, lax.rem(me + 1, n)).wait_recv()

    def sent(which, block):
        copy_to(which, 0, block, block, lax.rem(me + 1, n)).wait_send()

    def spread(which, key, src, dst):
        for p in range(1, n):
            peer = lax.rem(me + p, n)
            copy_to(which, key, src.at[peer], dst.at[me], peer).start()
        dst[me] = src[me]

    def put(ref, lead, ds, value, count, width):
        ref[(*lead, slice(None), slice(None), ds)] = value.reshape(count, width, lc).astype(BF16)

    def take(ref, lead, ds):
        block = ref[(*lead, slice(None), slice(None), ds)].astype(F32)
        return block.reshape(block.shape[0] * block.shape[1], lc)

    def to_slab(ref, lead, slab, slot, k):
        ds = lanes_of(k)
        width_c = ref.shape[-2]
        for s in range(ref.shape[-3]):
            block = ref[(*lead, s, slice(None), ds)].astype(F32)
            row = s * rows + k * crows
            for i in range(crows):
                part = block[:, i * res : (i + 1) * res]
                at = pl.ds(pl.multiple_of((row + i) * pitch + slot, 8), width_c)
                for t in range(tiles):
                    width = min(LANES, res - t * LANES)
                    slab[t, at, :width] = part[:, t * LANES : t * LANES + width]

    def matrix(slab, ch, count):
        at = pl.ds(ch, count, stride=pitch)
        pieces = [slab[t, at, :] for t in range(tiles)]
        whole = pieces[0] if tiles == 1 else jnp.concatenate(pieces, axis=1)
        return whole[:, :res].astype(BF16)

    def keep(slab, ch, value):
        count = value.shape[0]
        pad = tiles * LANES - res
        if pad:
            value = jnp.concatenate([value, jnp.zeros((count, pad), F32)], axis=1)
        for t in range(tiles):
            slab[t, pl.ds(ch, count, stride=pitch), :] = value[:, t * LANES : (t + 1) * LANES]

    def from_slab(slab, slot, ref, lead, k):
        width_c = ref.shape[-2]
        for s in range(ref.shape[-3]):
            row = s * rows + k * crows
            pieces = []
            for i in range(crows):
                at = pl.ds(pl.multiple_of((row + i) * pitch + slot, 8), width_c)
                for t in range(tiles):
                    width = min(LANES, res - t * LANES)
                    pieces.append(slab[t, at, :width])
            ref[(*lead, s, slice(None), lanes_of(k))] = jnp.concatenate(pieces, axis=1).astype(BF16)

    def early():
        return jnp.concatenate([acc_g[...], acc_f[...]], axis=1) * inv_count

    def hand_round(which, key, src, own, dst):
        summed = jnp.sum(src.astype(F32), axis=0).astype(BF16)
        own[...] = summed
        for p in range(1, n):
            copy_to(which, key, own, dst.at[me], lax.rem(me + p, n)).start()
        dst[me] = summed

    def level_near(key, rows_of, got):
        for p in range(1, m):
            slot = lax.rem(mine + p, m)
            copy_to(T_NEAR, key, rows_of.at[slot], got.at[mine], base + slot).start()
        got[mine] = rows_of[mine]

    def level_over(key, got, own, other):
        arrived(T_NEAR, key, got.at[pl.ds(0, m - 1)])
        own[...] = jnp.sum(got[...].astype(F32), axis=0).astype(BF16)
        copy_to(T_OVER, key, own, other, away + mine).start()

    def level_back(key, own, other, mean, back):
        arrived(T_OVER, key, other)
        mean[...] = (own[...].astype(F32) + other[...].astype(F32)).astype(BF16)
        for p in range(1, m):
            copy_to(T_BACK, key, mean, back.at[mine], base + lax.rem(mine + p, m)).start()
        back[mine] = mean[...]

    def level_sent(key_refs):
        for got, other, back in key_refs:
            sent(T_NEAR, got.at[pl.ds(0, m - 1)])
            sent(T_OVER, other)
            sent(T_BACK, back.at[pl.ds(0, m - 1)])

    for load in loads[:8]:
        load.wait()
    params = [embed[...], gain_on[...], gain_om[...], gain_in[...], gain_im[...]]
    cols[...] = jnp.concatenate(params + [jnp.zeros((2, c), F32)], axis=0).T
    here = lax.broadcasted_iota(jnp.int32, (rows, res), 1) == (
        lax.broadcasted_iota(jnp.int32, (rows, res), 0) + me * rows
    )
    row_mask = jnp.sum(jnp.where(here, residues[...], 0).astype(F32), axis=1, keepdims=True)
    row_chain = jnp.sum(jnp.where(here, chains[...], 0).astype(F32), axis=1, keepdims=True)
    both = row_mask * residues[...].astype(F32)
    same_chain = jnp.where(row_chain == chains[...].astype(F32), 1.0, 0.0)
    masks[0:1, :] = jnp.concatenate([both[i : i + 1] for i in range(rows)], axis=1)
    masks[1:2, :] = jnp.concatenate([same_chain[i : i + 1] for i in range(rows)], axis=1)
    emb0, emb1 = cols[:, 0:1], cols[:, 1:2]
    g_on, g_om, g_in, g_im = (cols[:, q : q + 1] for q in range(2, 6))
    loads[8].wait()

    def project(k):
        ds = lanes_of(k)
        same = masks[1:2, ds] > 0.5
        x = pair[ds, :].astype(F32).T + jnp.where(same, emb1, emb0)
        start[:, ds] = x
        hat, _ = norm_stats(x)
        nb = (hat * g_on).astype(BF16)
        normed[:, ds] = nb
        p = tn(out_proj[...], nb)
        pm = masks[0:1, ds]
        left = pm * sigmoid(p[:c]) * p[c : 2 * c]
        right = pm * sigmoid(p[2 * c : 3 * c]) * p[3 * c :]
        a_s[:, :, :, ds] = left.reshape(parts, m, hs, lc).astype(BF16)
        b_s[:, :, :, ds] = right.reshape(parts, m, hs, lc).astype(BF16)

    @pl.loop(0, chunks)
    def _(k):
        project(k)

    pl.semaphore_wait(barrier, n - 1)

    @pl.loop(0, parts)
    def _(h):
        near(A_OUT, h, a_s, a_r, (h,), pl.ds(0, total))
        far(B_OUT, h, b_s, b_r, (h,), pl.ds(0, total))

    for load in loads[9:]:
        load.wait()

    @pl.loop(0, chunks)
    def _(k):
        ds = lanes_of(k)
        gate[:, ds] = sigmoid(tn(out_gate[...], normed[:, ds]))
        cot_t[:, ds] = cot[ds, :].astype(F32).T

    def outgoing(h):
        arrived(A_OUT, h, a_r.at[h, pl.ds(0, m - 1)])

        @pl.loop(0, chunks)
        def _(k):
            to_slab(a_r, (h,), slab_a, h * hs, k)

        arrived(B_OUT, h, b_r.at[h, pl.ds(0, n - 1)])

        @pl.loop(0, chunks)
        def _(k):
            to_slab(b_r, (h,), slab_b, h * hs, k)

        for ch in range(hs):
            at = h * hs + ch
            keep(slab_o, at, nt(matrix(slab_a, at, half), matrix(slab_b, at, res)))

    @pl.loop(0, parts - 1)
    def _(h):
        outgoing(h)

        @pl.loop(0, chunks)
        def _(k):
            from_slab(slab_o, h * hs, x_s, (h,), k)

        near(X_OUT, h, x_s, x_r, (h,), pl.ds(0, total))

    outgoing(parts - 1)

    @pl.loop(0, chunks)
    def _(k):
        from_slab(slab_o, (parts - 1) * hs, x_s, (parts - 1,), k)
        near(X_OUT, parts - 1 + k, x_s, x_r, (parts - 1,), lanes_of(k))

    @pl.loop(0, parts - 1)
    def _(h):
        arrived(X_OUT, h, x_r.at[h, pl.ds(0, m - 1)])

    @pl.loop(0, chunks)
    def _(k):
        ds = lanes_of(k)
        arrived(X_OUT, parts - 1 + k, x_r.at[parts - 1, pl.ds(0, m - 1), :, ds])
        hat, _ = norm_stats(x_r[:, :, :, ds].astype(F32).reshape(c, lc))
        y = (hat * g_om).astype(BF16)
        v = (start[:, ds] + gate[:, ds] * tn(out_final[...], y)).astype(BF16)
        mid[:, ds] = v
        hat, _ = norm_stats(v.astype(F32))
        nb = (hat * g_in).astype(BF16)
        normed[:, ds] = nb
        p = tn(in_proj[...], nb)
        in_p[:, ds] = p
        pm = masks[0:1, ds]
        for q in range(2):
            value = pm * sigmoid(p[2 * q * c : (2 * q + 1) * c]) * p[(2 * q + 1) * c : (2 * q + 2) * c]
            put(abh_s, (q,), ds, value[every:], m, wh)
            if every:
                put(abe_s, (q,), ds, value[:every], n, we)
        near(AB_H, k, abh_s, abh_r, ALL, ds)
        if every:
            @pl.when(k > 0)
            def _():
                across(AB_E, k - 1, abe_s, abe_r, ALL, lanes_of(k - 1), True)

    if every:
        across(AB_E, chunks - 1, abe_s, abe_r, ALL, lanes_of(chunks - 1), True)

        @pl.loop(0, chunks)
        def _(k):
            across(AB_E, k, abe_s, abe_r, ALL, lanes_of(k), False)

    @pl.loop(0, chunks)
    def _(k):
        ds = lanes_of(k)
        s = sigmoid(tn(in_gate[...], normed[:, ds]))
        logit_s[:, ds] = s
        v = (cot_t[:, ds] * s).astype(BF16)
        gv[:, ds] = v
        gy[:, ds] = nn(in_final[...], v)

    acc_p[...] = jnp.zeros_like(acc_p)
    acc_g[...] = jnp.zeros_like(acc_g)
    acc_f[...] = jnp.zeros_like(acc_f)
    acc_n[...] = jnp.zeros_like(acc_n)
    acc_m[...] = jnp.zeros_like(acc_m)

    @pl.loop(0, chunks)
    def _(k):
        ds = lanes_of(k)
        arrived(AB_H, k, abh_r.at[:, pl.ds(0, m - 1), :, ds])
        to_slab(abh_r, (0,), slab_a, we, k)
        to_slab(abh_r, (1,), slab_b, we, k)

    for ch in range(wh):
        a = matrix(slab_a, we + ch, half)
        b = matrix(slab_b, we + ch, half)
        mat_a[ch] = a
        mat_b[ch] = b
        keep(slab_o, we + ch, tn(a, b))

    early_chunks = chunks - 1 if every else chunks

    @pl.loop(0, early_chunks)
    def _(k):
        from_slab(slab_o, we, xh_s, (), k)
        far(X_H, k, xh_s, xh_r, (), lanes_of(k), True)

    if every:
        from_slab(slab_o, we, xh_s, (), early_chunks)

        @pl.loop(0, chunks)
        def _(k):
            ds = lanes_of(k)
            arrived(AB_E, k, abe_r.at[:, pl.ds(0, n - 1), :, ds])
            to_slab(abe_r, (0,), slab_a, 0, k)
            to_slab(abe_r, (1,), slab_b, 0, k)

        for ch in range(we):
            a = matrix(slab_a, ch, res)
            b = matrix(slab_b, ch, res)
            mate_a[ch] = a
            mate_b[ch] = b
            keep(slab_o, ch, tn(a, b))

        def send_x(k):
            from_slab(slab_o, 0, xe_s, (), k)
            across(X_E, k, xe_s, xe_r, (), lanes_of(k), True)
            across(X_E, k, xe_s, xe_r, (), lanes_of(k), False)

        send_x(0)
        far(X_H, early_chunks, xh_s, xh_r, (), lanes_of(early_chunks), True)

        @pl.loop(1, chunks)
        def _(k):
            send_x(k)

    @pl.loop(0, chunks)
    def _(k):
        ds = lanes_of(k)
        arrived(X_H, k, xh_r.at[pl.ds(0, n - 1), :, ds])
        both = xh_r[pl.ds(0, m), :, ds].astype(F32) + xh_r[pl.ds(m, m), :, ds].astype(F32)
        x = both.reshape(c - every, lc)
        if every:
            arrived(X_E, k, xe_r.at[pl.ds(0, n - 1), :, ds])
            x = jnp.concatenate([take(xe_r, (), ds), x], axis=0)
        hat, inv = norm_stats(x)
        y = (hat * g_im).astype(BF16)
        value = tn(in_final[...], y)
        s = logit_s[:, ds]
        grad_l = (cot_t[:, ds] * value * s * (1.0 - s)).astype(BF16)
        gl[:, ds] = grad_l
        g = gy[:, ds]
        acc_m[...] += lane_sum(g * hat)
        grad_x = norm_back(g, hat, inv, g_im)
        put(gh_s, (), ds, grad_x[every:], m, wh)
        if every:
            put(ge_s, (), ds, grad_x[:every], n, we)
            across(G_E, k, ge_s, ge_r, (), ds, True)
            across(G_E, k, ge_s, ge_r, (), ds, False)
        else:
            far(G_H, k, gh_s, gh_r, (), ds)
        acc_f[...] += nt(y, gv[:, ds])

    if every:
        @pl.loop(0, chunks)
        def _(k):
            far(G_H, k, gh_s, gh_r, (), lanes_of(k))

    @pl.loop(0, chunks)
    def _(k):
        ds = lanes_of(k)
        grad_l = gl[:, ds]
        acc_g[...] += nt(normed[:, ds], grad_l)
        gy[:, ds] = nn(in_gate[...], grad_l)

    h_s[...] = early().reshape(m, c // m, 2 * c).astype(BF16)
    level_near(0, h_s, h_r)

    if every:
        @pl.loop(0, chunks)
        def _(k):
            arrived(G_E, k, ge_r.at[pl.ds(0, n - 1), :, lanes_of(k)])
            to_slab(ge_r, (), slab_a, 0, k)

        for ch in range(we):
            gx = matrix(slab_a, ch, res)
            keep(slab_o, ch, nt(mate_b[ch], gx))
            keep(slab_b, ch, nn(mate_a[ch], gx))

        @pl.loop(0, chunks)
        def _(k):
            ds = lanes_of(k)
            for q, slab in enumerate((slab_o, slab_b)):
                from_slab(slab, 0, de_s, (q,), k)
            across(D_E, k, de_s, de_r, ALL, ds, True)
            across(D_E, k, de_s, de_r, ALL, ds, False)

    @pl.loop(0, chunks)
    def _(k):
        arrived(G_H, k, gh_r.at[pl.ds(0, n - 1), :, lanes_of(k)])
        to_slab(gh_r, (), slab_a, we, k)

    for ch in range(wh):
        gx = matrix(slab_a, we + ch, res)
        keep(slab_o, we + ch, nt(mat_b[ch], gx))
        keep(slab_b, we + ch, nn(mat_a[ch], gx))

    @pl.loop(0, chunks)
    def _(k):
        for q, slab in enumerate((slab_o, slab_b)):
            from_slab(slab, we, dh_s, (q,), k)
        near(D_H, k, dh_s, dh_r, ALL, lanes_of(k))

    level_over(0, h_r, h_own, h_other)
    for g, (first, count) in enumerate(groups):
        @pl.loop(0, chunks)
        def _(k):
            ds = lanes_of(k)
            if first:
                arrived(D_H, k, dh_r.at[:, pl.ds(0, m - 1), :, ds])
                grads = [take(dh_r, (q,), ds) for q in range(2)]
            elif every:
                arrived(D_E, k, de_r.at[:, pl.ds(0, n - 1), :, ds])
                grads = [take(de_r, (q,), ds) for q in range(2)]
            else:
                arrived(D_H, k, dh_r.at[:, pl.ds(0, m - 1), :, ds])
                grads = [take(dh_r, (q,), ds) for q in range(2)]
            pm = masks[0:1, ds]
            blocks = []
            for q in range(2):
                s = sigmoid(in_p[pl.ds(2 * q * c + first, count), ds])
                scaled = grads[q] * pm * s
                blocks.append((scaled * in_p[pl.ds((2 * q + 1) * c + first, count), ds] * (1.0 - s)).astype(BF16))
                blocks.append(scaled.astype(BF16))
            for b in range(4):
                in_q[pl.ds(b * c + first, count), ds] = blocks[b]
            acc_p[g] += nt(normed[:, ds], jnp.concatenate(blocks, axis=0))

        if g == 0 and every:
            f_s[...] = (acc_p[g] * inv_count).reshape(m, c // m, 4 * count).astype(BF16)
            level_near(1, f_s, f_r)
            level_back(0, h_own, h_other, h_mean, h_back)
        else:
            g_s[...] = (acc_p[g] * inv_count).reshape(n, per, 4 * count).astype(BF16)
            spread(P_SUM, 0, g_s, g_r)
    if every:
        level_over(1, f_r, f_own, f_other)
    else:
        level_back(0, h_own, h_other, h_mean, h_back)

    @pl.loop(0, chunks)
    def _(k):
        ds = lanes_of(k)
        g = nn(in_proj[...], in_q[:, ds]) + gy[:, ds]
        hat, inv = norm_stats(mid[:, ds].astype(F32))
        acc_n[...] += lane_sum(g * hat)
        z = cot_t[:, ds] + norm_back(g, hat, inv, g_in)
        grad_out[ds, :] = z.T.astype(BF16)

    lane = lax.broadcasted_iota(jnp.int32, (c, LANES), 1)
    gains = jnp.where(lane == 0, acc_n[...], jnp.where(lane == 1, acc_m[...], 0.0))
    w_s[...] = (gains * inv_count).T[:2]
    for p in range(1, n):
        copy_to(GAINS, 0, w_s, w_r.at[me], lax.rem(me + p, n)).start()
    w_r[me] = w_s[...]
    if every:
        level_back(1, f_own, f_other, f_mean, f_back)
    arrived(P_SUM, 0, g_r.at[pl.ds(0, n - 1)])
    hand_round(P_ALL, 0, g_r[...], t_s, t_r)
    arrived(T_BACK, 0, h_back.at[pl.ds(0, m - 1)])
    both = h_back[...].astype(F32).reshape(c, 2 * c)
    gg_out[...] = both[:, :c]
    gf_out[...] = both[:, c:]
    arrived(GAINS, 0, w_r.at[pl.ds(0, n - 1)])
    gain_sums = jnp.sum(w_r[...], axis=0)
    gn_out[...] = gain_sums[0:1]
    gm_out[...] = gain_sums[1:2]

    for h in range(parts):
        sent(A_OUT, a_r.at[h, pl.ds(0, m - 1)])
        sent(B_OUT, b_r.at[h, pl.ds(0, n - 1)])
        sent(X_OUT, x_r.at[h, pl.ds(0, m - 1)])
    for q in range(2):
        sent(AB_H, abh_r.at[q, pl.ds(0, m - 1)])
        sent(D_H, dh_r.at[q, pl.ds(0, m - 1)])
    sent(X_H, xh_r.at[pl.ds(0, n - 1)])
    sent(G_H, gh_r.at[pl.ds(0, n - 1)])
    if every:
        for q in range(2):
            sent(AB_E, abe_r.at[q, pl.ds(0, n - 1)])
            sent(D_E, de_r.at[q, pl.ds(0, n - 1)])
        sent(X_E, xe_r.at[pl.ds(0, n - 1)])
        sent(G_E, ge_r.at[pl.ds(0, n - 1)])
    sent(GAINS, w_r.at[pl.ds(0, n - 1)])
    sent(P_SUM, g_r.at[pl.ds(0, n - 1)])
    level_sent([(h_r, h_other, h_back)] + ([(f_r, f_other, f_back)] if every else []))

    for g, (first, count) in enumerate(groups):
        if g == 0 and every:
            arrived(T_BACK, 1, f_back.at[pl.ds(0, m - 1)])
            whole = f_back[...].astype(F32).reshape(c, 4 * count)
        else:
            arrived(P_ALL, 0, t_r.at[pl.ds(0, n - 1)])
            sent(P_ALL, t_r.at[pl.ds(0, n - 1)])
            whole = t_r[...].astype(F32).reshape(c, 4 * count)
        for b in range(4):
            gp_out[:, b * c + first : b * c + first + count] = whole[:, b * count : (b + 1) * count]


def write_out(*refs):
    sems = refs[-1]
    copies = [pltpu.make_async_copy(refs[q], refs[q + 6], sems.at[q]) for q in range(6)]
    for copy in copies:
        copy.start()
    for copy in copies:
        copy.wait()


def shards(n, pair, cotangent, residue_mask, chain_ids, chain_embed, out_norm_gain, out_proj,
           out_gate, out_mid_gain, out_final, in_norm_gain, in_proj, in_gate, in_mid_gain, in_final):
    rows, res, c = pair.shape
    total = rows * res
    per = c // n
    lc = res * min(
        q for q in range(1, rows + 1)
        if rows % q == 0 and q * res % LANES == 0 and (rows // q <= 3)
    )
    tiles = -(-res // LANES)
    def full(dtype):
        return pltpu.VMEM((c, total), dtype)

    def block(*shape):
        return pltpu.VMEM((*shape, total), BF16)

    m = n // 2
    hc = c // m
    parts = hc // 8 if hc % 8 == 0 else 1
    every = c // 2 if (c // 2) % (8 * n) == 0 else 0
    we, wh = max(every // n, 8), (c - every) // m
    groups = 2 if every else 1
    wide = 4 * c // groups
    pitch = max(hc, every // n + wh) + PAD
    hs = hc // parts
    chunks = total // lc
    slab = pltpu.VMEM((tiles, res * pitch, LANES), F32)
    small = n if every else 1
    scratch = [
        pltpu.VMEM((total, c), BF16), pltpu.VMEM((total, c), BF16), pltpu.VMEM((1, res), jnp.int32), pltpu.VMEM((1, res), jnp.int32),
        pltpu.VMEM((2, c), F32),
    ] + [pltpu.VMEM((1, c), F32)] * 4 + [
        pltpu.VMEM((c, 4 * c), BF16), pltpu.VMEM((c, c), BF16), pltpu.VMEM((c, c), BF16),
        pltpu.VMEM((c, 4 * c), BF16), pltpu.VMEM((c, c), BF16), pltpu.VMEM((c, c), BF16),
        pltpu.VMEM((c, 8), F32), pltpu.VMEM((2, total), F32), pltpu.VMEM((4 * c, total), BF16), full(F32), full(BF16), full(F32),
        pltpu.VMEM((4 * c, total), F32), full(F32), full(BF16), full(F32), full(BF16), full(F32), full(BF16),
        block(parts, m, hs), block(parts, m, hs), block(parts, m, hs),
        block(parts, m, hs), block(parts, n, hs), block(parts, m, hs),
        block(2, m, wh), block(2, m, wh), block(n, wh), block(n, wh),
        block(m, wh), block(n, wh), block(2, m, wh), block(2, m, wh),
        block(2, small, we), block(2, small, we), block(small, we), block(small, we),
        block(small, we), block(small, we), block(2, small, we), block(2, small, we),
        slab, slab, slab,
        pltpu.VMEM((wh, m * rows, res), BF16), pltpu.VMEM((wh, m * rows, res), BF16),
        pltpu.VMEM((we, res, res), BF16), pltpu.VMEM((we, res, res), BF16),
        pltpu.VMEM((groups, c, wide), F32), pltpu.VMEM((c, c), F32), pltpu.VMEM((c, c), F32),
        pltpu.VMEM((c, 1), F32), pltpu.VMEM((c, 1), F32),
        pltpu.VMEM((n, per, wide), BF16), pltpu.VMEM((n, per, wide), BF16),
        pltpu.VMEM((per, wide), BF16), pltpu.VMEM((n, per, wide), BF16),
    ] + [
        pltpu.VMEM(shape, BF16) for w in (2 * c, wide)
        for shape in ((m, hc, w), (m, hc, w), (hc, w), (hc, w), (hc, w), (m, hc, w))
    ] + [
        pltpu.VMEM((2, c), F32), pltpu.VMEM((n, 2, c), F32),
        pltpu.SemaphoreType.DMA((15,)), pltpu.SemaphoreType.DMA((17,)), pltpu.SemaphoreType.DMA((receive_slots(parts, chunks)[-1],)),
    ]
    vmem = pl.BlockSpec(memory_space=pltpu.VMEM)
    results = pl.pallas_call(
        functools.partial(kernel, n, rows, res, lc, pitch, every),
        out_shape=(
            pltpu.VMEM((total, c), BF16),
            pltpu.VMEM((c, 4 * c), F32),
            pltpu.VMEM((c, c), F32),
            pltpu.VMEM((c, c), F32),
            pltpu.VMEM((1, c), F32),
            pltpu.VMEM((1, c), F32),
        ),
        in_specs=[pl.BlockSpec(memory_space=pl.ANY)] * 15,
        out_specs=(vmem,) * 6,
        scratch_shapes=scratch,
        compiler_params=pltpu.CompilerParams(
            collective_id=0, has_side_effects=True, vmem_limit_bytes=56 * 1024 * 1024
        ),
    )(
        pair.reshape(total, c), cotangent.reshape(total, c),
        residue_mask.reshape(1, res), chain_ids.reshape(1, res), chain_embed,
        out_norm_gain.reshape(1, c), out_mid_gain.reshape(1, c),
        in_norm_gain.reshape(1, c), in_mid_gain.reshape(1, c),
        out_proj, out_gate, out_final, in_proj, in_gate, in_final,
    )
    shapes = [((total, c), BF16), ((c, 4 * c), F32), ((c, c), F32), ((c, c), F32), ((1, c), F32), ((1, c), F32)]
    grad, gp, gg, gf, gn, gm = pl.pallas_call(
        write_out,
        out_shape=[jax.ShapeDtypeStruct(*shape) for shape in shapes],
        in_specs=[pl.BlockSpec(memory_space=pltpu.VMEM)] * 6,
        out_specs=[pl.BlockSpec(memory_space=pl.ANY)] * 6,
        scratch_shapes=[pltpu.SemaphoreType.DMA((6,))],
    )(*[pltpu.with_memory_space_constraint(r, pltpu.VMEM) for r in results])
    return grad.reshape(rows, res, c), gp, gg, gf, gn.reshape(c), gm.reshape(c)


def solution(mesh):
    split = P("dap", "cplx", None)
    return jax.shard_map(
        functools.partial(shards, mesh.shape["dap"]),
        mesh=mesh,
        in_specs=(split, split, P("cplx"), P("cplx")) + (P(),) * 11,
        out_specs=(split, P("cplx", None), P("cplx", None), P("cplx", None), P("cplx"), P("cplx")),
        check_vma=False,
    )
```

time: 78.6 us -> 73.5 us (0.935)
  Pallas kernels: 77.8 us -> 72.7 us
    pallas_call x1, Pallas kernels: 76.9 us -> 71.8 us  [shards(): pl.pallas_call(functools.partial(kernel, n, rows, res, lc, pitch, every),...]
where the time goes in v3:
time: 73.5 us; the launch traced here: 73.4 us
  Pallas kernels  72.7 us (99%)
    pallas_call x1, Pallas kernels, shards(): pl.pallas_call(functools.partial(kernel, n, rows, res, lc, pitch, every),...  71.8 us

profile of v3, /device:TPU:0, one launch (start us, length us, event | category | flops | bytes accessed | tf_op | source)
XLA Modules:
  0.0 73.4 jit_solution(1785735684620630322)
XLA Ops:
  0.6 71.8 %shard_map.190 = (bf16[1152,128]{1,0:T(8,128)(2,1)S(1)}, f32[128,512]{1,0:T(8,128)S(1)}, f32[128,128]{1,0:T(8,128)S(1)}, f32[128,128]{1,0:T(8,128)S(1)}, f32[1,128]{1,0:T(1,128)S(1)}, /*index=5*/f32[1,128]{1,0:T(1,128)S(1)}) custom-call(bf16[1152,128]{1,0:T(8,128)(2,1)} %bitcast.11, bf16[1152,128]{1,0:T(8,128)(2,1)} %bitcast.12, s32[1,96]{1,0:T(1,128)} %bitcast.13, ...), custom_call_target="tpu_custom_call" | custom-call | tf_op jit(solution)/shard_map/pallas_call | solution.py:658
  72.5 0.9 %shard_map.191 = (bf16[1152,128]{1,0:T(8,128)(2,1)}, f32[128,512]{1,0:T(8,128)}, f32[128,128]{1,0:T(8,128)}, f32[128,128]{1,0:T(8,128)}, f32[1,128]{1,0:T(1,128)}, /*index=5*/f32[1,128]{1,0:T(1,128)}) custom-call(bf16[1152,128]{1,0:T(8,128)(2,1)S(1)} %get-tuple-element.18.refs_0_, f32[128,512]{1,0:T(8,128)S(1)} %get-tuple-element.19.refs_1_, ...), custom_call_target="tpu_custom_call" | custom-call | tf_op jit(solution)/shard_map/pallas_call | solution.py:682

commit v4 on v3

--- a/solution.py
+++ b/solution.py
@@ -49,7 +49,7 @@
 
 
 def receive_slots(parts, chunks):
-    counts = [parts, parts, parts - 1 + chunks] + [chunks] * 8 + [1, 1, 1, 2, 2, 2]
+    counts = [parts, parts, parts - 1 + chunks] + [chunks] * 8 + [1, 2, 2, 1, 1, 1]
     return [sum(counts[:q]) for q in range(len(counts) + 1)]
 
 
@@ -66,7 +66,7 @@
     abe_s, abe_r, xe_s, xe_r, ge_s, ge_r, de_s, de_r,
     slab_a, slab_b, slab_o, mat_a, mat_b, mate_a, mate_b,
     acc_p, acc_g, acc_f, acc_n, acc_m, g_s, g_r, t_s, t_r,
-    h_s, h_r, h_own, h_other, h_mean, h_back, f_s, f_r, f_own, f_other, f_mean, f_back, w_s, w_r,
+    h_s, h_r, h_own, h_other, h_mean, h_back, f_s, f_r, f_own, f_back, w_s, w_r,
     in_sem, send_sem, recv_sem,
 ):
     me = lax.axis_index("dap")
@@ -143,12 +143,6 @@
     def sent(which, block):
         copy_to(which, 0, block, block, lax.rem(me + 1, n)).wait_send()
 
-    def spread(which, key, src, dst):
-        for p in range(1, n):
-            peer = lax.rem(me + p, n)
-            copy_to(which, key, src.at[peer], dst.at[me], peer).start()
-        dst[me] = src[me]
-
     def put(ref, lead, ds, value, count, width):
         ref[(*lead, slice(None), slice(None), ds)] = value.reshape(count, width, lc).astype(BF16)
 
@@ -198,12 +192,39 @@
     def early():
         return jnp.concatenate([acc_g[...], acc_f[...]], axis=1) * inv_count
 
-    def hand_round(which, key, src, own, dst):
-        summed = jnp.sum(src.astype(F32), axis=0).astype(BF16)
-        own[...] = summed
-        for p in range(1, n):
-            copy_to(which, key, own, dst.at[me], lax.rem(me + p, n)).start()
-        dst[me] = summed
+    first_mid = n // 4
+    in_middle = (me >= first_mid) & (me < first_mid + m)
+
+    def middle_sum(key, src, got):
+        for r in range(m):
+            @pl.when(me != first_mid + r)
+            def _():
+                copy_to(P_SUM, key, src.at[r], got.at[me], first_mid + r).start()
+
+        @pl.when(in_middle)
+        def _():
+            got[me] = src[me - first_mid]
+
+    def middle_round(key, got, own, back):
+        @pl.when(in_middle)
+        def _():
+            arrived(P_SUM, key, got.at[pl.ds(0, n - 1)])
+            own[...] = jnp.sum(got[...].astype(F32), axis=0).astype(BF16)
+            for p in range(1, n):
+                copy_to(P_ALL, key, own, back.at[me - first_mid], lax.rem(me + p, n)).start()
+            back[me - first_mid] = own[...]
+
+    def middle_done(key, got, back):
+        @pl.when(in_middle)
+        def _():
+            arrived(P_ALL, key, back.at[pl.ds(0, m - 1)])
+            sent(P_SUM, back.at[pl.ds(0, m - 1)])
+            sent(P_ALL, got.at[pl.ds(0, n - 1)])
+
+        @pl.when(jnp.logical_not(in_middle))
+        def _():
+            arrived(P_ALL, key, back)
+            sent(P_SUM, back)
 
     def level_near(key, rows_of, got):
         for p in range(1, m):
@@ -494,41 +515,42 @@
         near(D_H, k, dh_s, dh_r, ALL, lanes_of(k))
 
     level_over(0, h_r, h_own, h_other)
-    for g, (first, count) in enumerate(groups):
-        @pl.loop(0, chunks)
-        def _(k):
-            ds = lanes_of(k)
-            if first:
-                arrived(D_H, k, dh_r.at[:, pl.ds(0, m - 1), :, ds])
-                grads = [take(dh_r, (q,), ds) for q in range(2)]
-            elif every:
-                arrived(D_E, k, de_r.at[:, pl.ds(0, n - 1), :, ds])
-                grads = [take(de_r, (q,), ds) for q in range(2)]
-            else:
-                arrived(D_H, k, dh_r.at[:, pl.ds(0, m - 1), :, ds])
-                grads = [take(dh_r, (q,), ds) for q in range(2)]
-            pm = masks[0:1, ds]
-            blocks = []
-            for q in range(2):
-                s = sigmoid(in_p[pl.ds(2 * q * c + first, count), ds])
-                scaled = grads[q] * pm * s
-                blocks.append((scaled * in_p[pl.ds((2 * q + 1) * c + first, count), ds] * (1.0 - s)).astype(BF16))
-                blocks.append(scaled.astype(BF16))
-            for b in range(4):
-                in_q[pl.ds(b * c + first, count), ds] = blocks[b]
-            acc_p[g] += nt(normed[:, ds], jnp.concatenate(blocks, axis=0))
-
+    def finish(g, k):
+        first, count = groups[g]
+        ds = lanes_of(k)
         if g == 0 and every:
-            f_s[...] = (acc_p[g] * inv_count).reshape(m, c // m, 4 * count).astype(BF16)
-            level_near(1, f_s, f_r)
-            level_back(0, h_own, h_other, h_mean, h_back)
+            arrived(D_E, k, de_r.at[:, pl.ds(0, n - 1), :, ds])
+            grads = [take(de_r, (q,), ds) for q in range(2)]
         else:
-            g_s[...] = (acc_p[g] * inv_count).reshape(n, per, 4 * count).astype(BF16)
-            spread(P_SUM, 0, g_s, g_r)
+            arrived(D_H, k, dh_r.at[:, pl.ds(0, m - 1), :, ds])
+            grads = [take(dh_r, (q,), ds) for q in range(2)]
+        pm = masks[0:1, ds]
+        blocks = []
+        for q in range(2):
+            s = sigmoid(in_p[pl.ds(2 * q * c + first, count), ds])
+            scaled = grads[q] * pm * s
+            blocks.append((scaled * in_p[pl.ds((2 * q + 1) * c + first, count), ds] * (1.0 - s)).astype(BF16))
+            blocks.append(scaled.astype(BF16))
+        for b in range(4):
+            in_q[pl.ds(b * c + first, count), ds] = blocks[b]
+        acc_p[g] += nt(normed[:, ds], jnp.concatenate(blocks, axis=0))
+
+    last = len(groups) - 1
     if every:
-        level_over(1, f_r, f_own, f_other)
-    else:
-        level_back(0, h_own, h_other, h_mean, h_back)
+        @pl.loop(0, chunks)
+        def _(k):
+            finish(0, k)
+
+        f_s[...] = (acc_p[0] * inv_count).reshape(m, c // m, 2 * c).astype(BF16)
+        middle_sum(1, f_s, f_r)
+
+    @pl.loop(0, chunks)
+    def _(k):
+        finish(last, k)
+
+    g_s[...] = (acc_p[last] * inv_count).reshape(m, c // m, 4 * groups[last][1]).astype(BF16)
+    middle_sum(0, g_s, g_r)
+    level_back(0, h_own, h_other, h_mean, h_back)
 
     @pl.loop(0, chunks)
     def _(k):
@@ -546,9 +568,8 @@
         copy_to(GAINS, 0, w_s, w_r.at[me], lax.rem(me + p, n)).start()
     w_r[me] = w_s[...]
     if every:
-        level_back(1, f_own, f_other, f_mean, f_back)
-    arrived(P_SUM, 0, g_r.at[pl.ds(0, n - 1)])
-    hand_round(P_ALL, 0, g_r[...], t_s, t_r)
+        middle_round(1, f_r, f_own, f_back)
+    middle_round(0, g_r, t_s, t_r)
     arrived(T_BACK, 0, h_back.at[pl.ds(0, m - 1)])
     both = h_back[...].astype(F32).reshape(c, 2 * c)
     gg_out[...] = both[:, :c]
@@ -574,16 +595,14 @@
         sent(X_E, xe_r.at[pl.ds(0, n - 1)])
         sent(G_E, ge_r.at[pl.ds(0, n - 1)])
     sent(GAINS, w_r.at[pl.ds(0, n - 1)])
-    sent(P_SUM, g_r.at[pl.ds(0, n - 1)])
-    level_sent([(h_r, h_other, h_back)] + ([(f_r, f_other, f_back)] if every else []))
+    level_sent([(h_r, h_other, h_back)])
 
     for g, (first, count) in enumerate(groups):
         if g == 0 and every:
-            arrived(T_BACK, 1, f_back.at[pl.ds(0, m - 1)])
+            middle_done(1, f_r, f_back)
             whole = f_back[...].astype(F32).reshape(c, 4 * count)
         else:
-            arrived(P_ALL, 0, t_r.at[pl.ds(0, n - 1)])
-            sent(P_ALL, t_r.at[pl.ds(0, n - 1)])
+            middle_done(0, g_r, t_r)
             whole = t_r[...].astype(F32).reshape(c, 4 * count)
         for b in range(4):
             gp_out[:, b * c + first : b * c + first + count] = whole[:, b * count : (b + 1) * count]
@@ -645,11 +664,13 @@
         pltpu.VMEM((we, res, res), BF16), pltpu.VMEM((we, res, res), BF16),
         pltpu.VMEM((groups, c, wide), F32), pltpu.VMEM((c, c), F32), pltpu.VMEM((c, c), F32),
         pltpu.VMEM((c, 1), F32), pltpu.VMEM((c, 1), F32),
-        pltpu.VMEM((n, per, wide), BF16), pltpu.VMEM((n, per, wide), BF16),
-        pltpu.VMEM((per, wide), BF16), pltpu.VMEM((n, per, wide), BF16),
+        pltpu.VMEM((m, hc, wide), BF16), pltpu.VMEM((n, hc, wide), BF16),
+        pltpu.VMEM((hc, wide), BF16), pltpu.VMEM((m, hc, wide), BF16),
     ] + [
-        pltpu.VMEM(shape, BF16) for w in (2 * c, wide)
-        for shape in ((m, hc, w), (m, hc, w), (hc, w), (hc, w), (hc, w), (m, hc, w))
+        pltpu.VMEM(shape, BF16)
+        for shape in ((m, hc, 2 * c), (m, hc, 2 * c), (hc, 2 * c), (hc, 2 * c), (hc, 2 * c), (m, hc, 2 * c))
+    ] + [
+        pltpu.VMEM(shape, BF16) for shape in ((m, hc, wide), (n, hc, wide), (hc, wide), (m, hc, wide))
     ] + [
         pltpu.VMEM((2, c), F32), pltpu.VMEM((n, 2, c), F32),
         pltpu.SemaphoreType.DMA((15,)), pltpu.SemaphoreType.DMA((17,)), pltpu.SemaphoreType.DMA((receive_slots(parts, chunks)[-1],)),

time: 73.5 us -> 72.1 us (0.981)
  Pallas kernels: 72.7 us -> 71.3 us
    pallas_call x1, Pallas kernels: 71.8 us -> 70.4 us  [shards(): pl.pallas_call(functools.partial(kernel, n, rows, res, lc, pitch, every),...]
where the time goes in v4:
time: 72.1 us; the launch traced here: 71.9 us
  Pallas kernels  71.3 us (99%)
    pallas_call x1, Pallas kernels, shards(): pl.pallas_call(functools.partial(kernel, n, rows, res, lc, pitch, every),...  70.4 us

profile of v4, /device:TPU:0, one launch (start us, length us, event | category | flops | bytes accessed | tf_op | source)
XLA Modules:
  0.0 71.9 jit_solution(836891718798865648)
XLA Ops:
  0.6 70.4 %shard_map.190 = (bf16[1152,128]{1,0:T(8,128)(2,1)S(1)}, f32[128,512]{1,0:T(8,128)S(1)}, f32[128,128]{1,0:T(8,128)S(1)}, f32[128,128]{1,0:T(8,128)S(1)}, f32[1,128]{1,0:T(1,128)S(1)}, /*index=5*/f32[1,128]{1,0:T(1,128)S(1)}) custom-call(bf16[1152,128]{1,0:T(8,128)(2,1)} %bitcast.11, bf16[1152,128]{1,0:T(8,128)(2,1)} %bitcast.12, s32[1,96]{1,0:T(1,128)} %bitcast.13, ...), custom_call_target="tpu_custom_call" | custom-call | tf_op jit(solution)/shard_map/pallas_call | solution.py:679
  71.0 0.9 %shard_map.191 = (bf16[1152,128]{1,0:T(8,128)(2,1)}, f32[128,512]{1,0:T(8,128)}, f32[128,128]{1,0:T(8,128)}, f32[128,128]{1,0:T(8,128)}, f32[1,128]{1,0:T(1,128)}, /*index=5*/f32[1,128]{1,0:T(1,128)}) custom-call(bf16[1152,128]{1,0:T(8,128)(2,1)S(1)} %get-tuple-element.18.refs_0_, f32[128,512]{1,0:T(8,128)S(1)} %get-tuple-element.19.refs_1_, ...), custom_call_target="tpu_custom_call" | custom-call | tf_op jit(solution)/shard_map/pallas_call | solution.py:703

commit v5 on v4

--- a/solution.py
+++ b/solution.py
@@ -361,12 +361,12 @@
                 put(abe_s, (q,), ds, value[:every], n, we)
         near(AB_H, k, abh_s, abh_r, ALL, ds)
         if every:
-            @pl.when(k > 0)
-            def _():
-                across(AB_E, k - 1, abe_s, abe_r, ALL, lanes_of(k - 1), True)
+            pass
 
     if every:
-        across(AB_E, chunks - 1, abe_s, abe_r, ALL, lanes_of(chunks - 1), True)
+        @pl.loop(0, chunks)
+        def _(k):
+            across(AB_E, k, abe_s, abe_r, ALL, lanes_of(k), True)
 
         @pl.loop(0, chunks)
         def _(k):
@@ -459,12 +459,15 @@
         if every:
             put(ge_s, (), ds, grad_x[:every], n, we)
             across(G_E, k, ge_s, ge_r, (), ds, True)
-            across(G_E, k, ge_s, ge_r, (), ds, False)
         else:
             far(G_H, k, gh_s, gh_r, (), ds)
         acc_f[...] += nt(y, gv[:, ds])
 
     if every:
+        @pl.loop(0, chunks)
+        def _(k):
+            across(G_E, k, ge_s, ge_r, (), lanes_of(k), False)
+
         @pl.loop(0, chunks)
         def _(k):
             far(G_H, k, gh_s, gh_r, (), lanes_of(k))

time: 72.1 us -> 72 us (level)
  no operation moved by 1% of the time
where the time goes in v5:
time: 72 us; the launch traced here: 71.9 us
  Pallas kernels  71.2 us (99%)
    pallas_call x1, Pallas kernels, shards(): pl.pallas_call(functools.partial(kernel, n, rows, res, lc, pitch, every),...  70.3 us

profile of v5, /device:TPU:0, one launch (start us, length us, event | category | flops | bytes accessed | tf_op | source)
XLA Modules:
  0.0 71.9 jit_solution(8034304979715040883)
XLA Ops:
  0.6 70.3 %shard_map.190 = (bf16[1152,128]{1,0:T(8,128)(2,1)S(1)}, f32[128,512]{1,0:T(8,128)S(1)}, f32[128,128]{1,0:T(8,128)S(1)}, f32[128,128]{1,0:T(8,128)S(1)}, f32[1,128]{1,0:T(1,128)S(1)}, /*index=5*/f32[1,128]{1,0:T(1,128)S(1)}) custom-call(bf16[1152,128]{1,0:T(8,128)(2,1)} %bitcast.11, bf16[1152,128]{1,0:T(8,128)(2,1)} %bitcast.12, s32[1,96]{1,0:T(1,128)} %bitcast.13, ...), custom_call_target="tpu_custom_call" | custom-call | tf_op jit(solution)/shard_map/pallas_call | solution.py:682
  71.0 0.9 %shard_map.191 = (bf16[1152,128]{1,0:T(8,128)(2,1)}, f32[128,512]{1,0:T(8,128)}, f32[128,128]{1,0:T(8,128)}, f32[128,128]{1,0:T(8,128)}, f32[1,128]{1,0:T(1,128)}, /*index=5*/f32[1,128]{1,0:T(1,128)}) custom-call(bf16[1152,128]{1,0:T(8,128)(2,1)S(1)} %get-tuple-element.18.refs_0_, f32[128,512]{1,0:T(8,128)S(1)} %get-tuple-element.19.refs_1_, ...), custom_call_target="tpu_custom_call" | custom-call | tf_op jit(solution)/shard_map/pallas_call | solution.py:706
